TPU v7x, 128 devices: a whole 4x4x4 slice. The times are simulated.
128 devices in a mesh: dp: 64 (over z, y, x), mp: 2 (over core).
Axes of the slice: x: 4, y: 4, z: 4, core: 2. Of those that a mesh axis runs over, the one named last changes fastest.
Arguments:
- hot_rows: int32 [64, 64, 32], P('dp'), may hold values from 0 to 4095
- hot_count: int32 [64, 64], P('dp'), may hold values from 1 to 32, as said below
- hot_cot: bfloat16 [64, 64, 32, 128], P('dp'), may hold values from -6 to 6
- table: float32 [262144, 128], P('dp'), may hold values from -3 to 3
- cold_ids: int32 [65536], P('dp'), may hold values from 0 to 1048575
- hash_mult: int32 [1024], replicated, may hold values from 1 to 1023
- hash_add: int32 [1024], replicated, may hold values from 0 to 1000002
- layer_one: bfloat16 [1024, 1024], P(None, 'mp'), may hold values from -0.1875 to 0.1875
- layer_two: bfloat16 [1024, 1024], P('mp'), may hold values from -0.1875 to 0.1875
- layer_three: bfloat16 [1024, 1024], P(None, 'mp'), may hold values from -0.1875 to 0.1875
- layer_four: bfloat16 [1024, 128], P('mp'), may hold values from -0.1875 to 0.1875
- cold_cot: bfloat16 [65536, 128], P('dp'), may hold values from -6 to 6
Outputs:
- hot_emb: bfloat16 [64, 64, 32, 128], P('dp')
- new_table: float32 [262144, 128], P('dp')
- cold_emb: bfloat16 [65536, 128], P('dp')
- grad_one: float32 [1024, 1024], P(None, 'mp')
- grad_two: float32 [1024, 1024], P('mp')
- grad_three: float32 [1024, 1024], P(None, 'mp')
- grad_four: float32 [1024, 128], P('mp')
Inputs may be any that keep to these rules, and one draw needn't show every extreme that they name: `hot_rows`: entries index the owner's block of 4096 rows; entries in unused slots are arbitrary. `hot_count`: every batch shard fills all 32 slots of some owner, and some owner receives 32 from every batch shard.
All inputs are finite; a program needn't handle non-finite values.
Results may differ from a plain program's by a relative error of at most 0.0074.
Values may be sent and summed in bfloat16 or wider, within the bound.
A program may use at most 128 MiB of HBM per device.

v0:
```python
import jax
import jax.numpy as jnp
from jax import lax
from jax.sharding import PartitionSpec as P

COLD = 1024


learn_rate = 0.5
modulus = 1000003


def over_pieces(array, axis):
    return lax.all_gather(array, axis).sum(0)


def from_everyone(array, axis):
    size = lax.axis_size(axis)
    return lax.all_to_all(
        jnp.broadcast_to(array[None], (size, *array.shape)), axis, 0, 0, tiled=True
    )


def over_copies(array, axis):
    everything = from_everyone(array, axis)
    return jnp.sum(everything, axis=0)


def in_order(tiles, dim):
    dims = list(tiles.shape[1:])
    dims[dim] *= tiles.shape[0]
    return jnp.moveaxis(tiles, 0, dim).reshape(dims)


def gather_directly(array, axis, dim):
    return in_order(from_everyone(array, axis), dim)


def features_of(ids, hash_mult, hash_add):
    hashed = jnp.remainder(ids[:, None] * hash_mult[None, :] + hash_add[None, :], modulus)
    return (hashed.astype(jnp.float32) * (2.0 / 1000002.0) - 1.0).astype(jnp.bfloat16)


def silu_grad(value):
    sig = jax.nn.sigmoid(value)
    return sig * (1.0 + value * (1.0 - sig))


def local(
    hot_rows,
    hot_count,
    hot_cot,
    table,
    cold_ids,
    hash_mult,
    hash_add,
    layer_one,
    layer_two,
    layer_three,
    layer_four,
    cold_cot,
):
    width = table.shape[1]
    slots_all = hot_rows.shape[2]
    span = slots_all // lax.axis_size("mp")
    begin = lax.axis_index("mp") * span
    mine = lax.dynamic_slice_in_dim(hot_rows, begin, span, 2)
    received = lax.all_to_all(mine, "dp", split_axis=1, concat_axis=1, tiled=True)
    fetched = jnp.take(table, received.reshape(-1), axis=0).astype(jnp.bfloat16)
    fetched = fetched.reshape(received.shape + (width,))
    returned = lax.all_to_all(fetched, "dp", split_axis=1, concat_axis=1, tiled=True)
    returned, received = (returned, received)
    feats = features_of(cold_ids, hash_mult, hash_add)
    pre_one = jnp.dot(feats, layer_one, preferred_element_type=jnp.float32)
    act_one = jax.nn.silu(pre_one).astype(jnp.bfloat16)
    pre_two = over_pieces(jnp.dot(act_one, layer_two, preferred_element_type=jnp.float32), "mp")
    act_two = jax.nn.silu(pre_two).astype(jnp.bfloat16)
    pre_three = jnp.dot(act_two, layer_three, preferred_element_type=jnp.float32)
    act_three = jax.nn.silu(pre_three).astype(jnp.bfloat16)
    cold_emb = over_copies(
        jnp.dot(act_three, layer_four, preferred_element_type=jnp.float32), "mp"
    ).astype(jnp.bfloat16)
    slot_index = begin + jnp.arange(span, dtype=jnp.int32)
    used = slot_index[None, None, :] < hot_count[:, :, None]
    own_emb = jnp.where(used[..., None], returned, jnp.zeros_like(returned))
    own_cot = lax.dynamic_slice_in_dim(hot_cot, begin, span, 2)
    own_cot = jnp.where(used[..., None], own_cot, jnp.zeros_like(own_cot))
    arrived = lax.all_to_all(own_cot, "dp", split_axis=1, concat_axis=1, tiled=True)
    factor = float(COLD * lax.axis_size("dp")) ** (-0.5)
    back_three = (
        jnp.dot(cold_cot, layer_four.T, preferred_element_type=jnp.float32) * silu_grad(pre_three)
    ).astype(jnp.bfloat16)
    part_four = jnp.dot(act_three.T, cold_cot, preferred_element_type=jnp.float32) * factor
    back_sum = over_pieces(
        jnp.dot(back_three, layer_three.T, preferred_element_type=jnp.float32), "mp"
    )
    part_three = jnp.dot(act_two.T, back_three, preferred_element_type=jnp.float32) * factor
    back_two = (back_sum * silu_grad(pre_two)).astype(jnp.bfloat16)
    part_two = jnp.dot(act_one.T, back_two, preferred_element_type=jnp.float32) * factor
    back_one = (
        jnp.dot(back_two, layer_two.T, preferred_element_type=jnp.float32) * silu_grad(pre_one)
    ).astype(jnp.bfloat16)
    part_one = jnp.dot(feats.T, back_one, preferred_element_type=jnp.float32) * factor
    part_one, part_two, part_three, part_four = lax.psum(
        (part_one, part_two, part_three, part_four), "dp"
    )
    arrived = gather_directly(arrived, "mp", 2)
    received = gather_directly(received, "mp", 2)
    hot_emb = gather_directly(own_emb, "mp", 2)
    delta = (
        jnp.zeros_like(table)
        .at[received.reshape(-1)]
        .add(arrived.reshape(-1, width).astype(jnp.float32))
    )
    new_table = table - learn_rate * delta
    return (hot_emb, new_table, cold_emb, part_one, part_two, part_three, part_four)


def solution(mesh):
    in_specs = (
        P("dp", None, None),
        P("dp", None),
        P("dp", None, None, None),
        P("dp", None),
        P("dp"),
        P(),
        P(),
        P(None, "mp"),
        P("mp", None),
        P(None, "mp"),
        P("mp", None),
        P("dp", None),
    )
    out_specs = (
        P("dp", None, None, None),
        P("dp", None),
        P("dp", None),
        P(None, "mp"),
        P("mp", None),
        P(None, "mp"),
        P("mp", None),
    )
    return jax.shard_map(local, mesh=mesh, in_specs=in_specs, out_specs=out_specs, check_vma=False)
```

profile of v0, /device:TPU:0, one launch (start us, length us, event | category | flops | bytes accessed | tf_op | source)
XLA Modules:
  0.0 269.6 jit_solution(9633521886486711486)
XLA Ops:
  7.2 4.8 %fusion.9 = f32[1024,512]{1,0:T(8,128)S(1)} fusion(bf16[1024,512]{1,0:T(8,128)(2,1)} %param.19, s32[1024]{0:T(1024)} %param.18, s32[1024]{0:T(1024)} %param.17, s32[1024]{0:T(1024)} %param.16), kind=kOutput, calls=%fused_computation.21 | convolution fusion | flops 1086324736 | bytes 3158016 | tf_op jit(solution)/shard_map/dot_general | solution.py:74
  12.0 1.3 copy-done.19
  13.4 3.3 %fusion.25 = f32[1024,1024]{1,0:T(8,128)} fusion(bf16[512,1024]{1,0:T(8,128)(2,1)S(1)} %copy-done.14, f32[1024,512]{1,0:T(8,128)S(1)} %fusion.9), kind=kOutput, calls=%fused_computation.50 | convolution fusion | flops 1076363264 | bytes 7340032 | tf_op jit(solution)/shard_map/dot_general | solution.py:76
  16.7 25.1 %all-gather.5.cloned.1.call-done = f32[2048,1024]{1,0:T(8,128)} async-done(((f32[1024,1024]{1,0:T(8,128)}), f32[2048,1024]{1,0:T(8,128)}) %all-gather.5.cloned.1.call-update) | async-done | bytes 8388624 | tf_op jit(solution)/shard_map/all_gather | solution.py:14
  41.8 6.7 %reduce_sum.27 = f32[1024,1024]{1,0:T(8,128)} reduce(f32[2,1024,1024]{2,1,0:T(8,128)} %bitcast.44, f32[]{:T(128)} %constant.31.clone.1), dimensions={0}, to_apply=%region_1.2 | reduce | flops 1048576 | bytes 12582916 | tf_op jit(solution)/shard_map/reduce_sum | solution.py:14
  48.5 3.3 %multiply_convert_fusion.1 = bf16[1024,1024]{1,0:T(8,128)(2,1)S(1)} fusion(f32[1024,1024]{1,0:T(8,128)} %reduce_sum.27), kind=kLoop, calls=%fused_computation.8 | loop fusion | flops 5242880 | bytes 6291456 | tf_op jit(solution)/shard_map/convert_element_type | solution.py:77
  51.8 1.5 multiply_convert_fusion.4
  53.4 0.9 multiply_convert_fusion.3
  54.3 3.2 %fusion.27 = f32[1024,1024]{1,0:T(8,128)} fusion(bf16[1024,512]{1,0:T(8,128)(2,1)S(1)} %multiply_convert_fusion.3, bf16[1024,512]{1,0:T(8,128)(2,1)S(1)} %copy-done), kind=kOutput, calls=%fused_computation.54 | convolution fusion | flops 1073741824 | bytes 6291456 | tf_op jit(solution)/shard_map/dot_general | solution.py:95
  57.8 1.2 convolution_multiply_fusion.2
  59.0 4.2 %convolution_multiply_fusion = f32[1024,512]{1,0:T(8,128)} fusion(bf16[1024,1024]{1,0:T(8,128)(2,1)} %copy-done.5, bf16[1024,512]{1,0:T(8,128)(2,1)S(1)} %multiply_convert_fusion.3), kind=kOutput, calls=%fused_computation.23 | convolution fusion | flops 1074266112 | bytes 5242880 | tf_op jit(solution)/shard_map/dot_general | solution.py:97
  63.2 18.4 %all-gather.7.cloned.1.call-done = f32[2048,1024]{1,0:T(8,128)} async-done(((f32[1024,1024]{1,0:T(8,128)}), f32[2048,1024]{1,0:T(8,128)}) %all-gather.7.cloned.1.call-update) | async-done | bytes 8388624 | tf_op jit(solution)/shard_map/all_gather | solution.py:14
  81.6 6.6 %reduce_sum.29 = f32[1024,1024]{1,0:T(8,128)} reduce(f32[2,1024,1024]{2,1,0:T(8,128)} %bitcast.43, f32[]{:T(128)} %constant.31.clone.1), dimensions={0}, to_apply=%region_3.4 | reduce | flops 1048576 | bytes 12582916 | tf_op jit(solution)/shard_map/reduce_sum | solution.py:14
  88.2 5.0 %multiply_convert_fusion = bf16[1024,1024]{1,0:T(8,128)(2,1)S(1)} fusion(f32[1024,1024]{1,0:T(8,128)} %reduce_sum.29, f32[1024,1024]{1,0:T(8,128)} %reduce_sum.27), kind=kLoop, calls=%fused_computation.7 | loop fusion | flops 9437184 | bytes 10485760 | tf_op jit(solution)/shard_map/convert_element_type | solution.py:98
  93.4 2.6 convolution_multiply_fusion.1
  96.0 8.1 %fusion.11 = f32[1024,512]{1,0:T(8,128)} fusion(s32[1024]{0:T(1024)S(1)} %copy-done.16, s32[1024]{0:T(1024)S(1)} %copy-done.17, s32[1024]{0:T(1024)S(1)} %copy-done.18, f32[1024,512]{1,0:T(8,128)} %copy-done.19, bf16[1024,1024]{1,0:T(8,128)(2,1)S(1)} %multiply_convert_fusion, bf16[512,1024]{1,0:T(8,128)(2,1)S(1)} %copy-done.15), kind=kOutput, calls=%fused_computation.25 | convolution fusion | flops 2165309440 | bytes 7352320 | tf_op jit(solution)/shard_map/dot_general | solution.py:103
  104.2 0.7 copy-done.12
  104.8 0.7 copy.43
  105.5 10.4 %all-to-all-start = ((s32[1,64,16]{2,0,1:T(1,128)}), s32[1,64,16]{2,0,1:T(1,128)S(1)}, u32[]{:S(2)}, u32[]{:S(2)}) async-start(s32[1,64,16]{2,0,1:T(1,128)} %copy.43), calls=%async_computation | async-start | bytes 65536 | tf_op jit(solution)/shard_map/all_to_all | solution.py:68
  116.0 9.8 %all-to-all-done = s32[1,64,16]{2,0,1:T(1,128)S(1)} async-done(((s32[1,64,16]{2,0,1:T(1,128)}), s32[1,64,16]{2,0,1:T(1,128)S(1)}, u32[]{:S(2)}, u32[]{:S(2)}) %all-to-all-start) | async-done | bytes 4128 | tf_op jit(solution)/shard_map/all_to_all | solution.py:68
  125.8 0.7 reshape.200
  126.5 3.4 %all-to-all-start.3 = ((s32[2,1,1024]{2,1,0:T(1,128)}), s32[2,1,1024]{2,1,0:T(1,128)S(1)}, u32[]{:S(2)}, u32[]{:S(2)}) async-start(s32[2,1,1024]{2,1,0:T(1,128)} %reshape.200), calls=%async_computation.3 | async-start | bytes 16384 | tf_op jit(solution)/shard_map/all_to_all | solution.py:19
  130.0 0.5 broadcast.139
  130.5 0.7 reduce.3
  131.4 2.9 %gather_fusion = bf16[1024,128]{1,0:T(8,128)(2,1)S(1)} fusion(f32[4096,128]{1,0:T(8,128)S(1)} %copy-done.2, s32[1024]{0:T(1024)S(1)} %broadcast_clamp_fusion), kind=kCustom, calls=%fused_computation | custom fusion | bytes 528384 | tf_op jit(solution)/shard_map/jit(_take)/gather | solution.py:69
  134.3 0.9 select_convert_fusion
  135.2 4.9 %all-to-all-start.1 = ((bf16[1,64,16,128]{3,2,0,1:T(8,128)(2,1)}), bf16[1,64,16,128]{3,2,0,1:T(8,128)(2,1)S(1)}, u32[]{:S(2)}, u32[]{:S(2)}) async-start(bf16[1,64,16,128]{3,2,0,1:T(8,128)(2,1)} %select_convert_fusion), calls=%async_computation.1 | async-start | bytes 524288 | tf_op jit(solution)/shard_map/all_to_all | solution.py:71
  140.2 0.5 broadcast.140
  140.7 0.7 reduce.4
  141.7 9.4 %all-to-all-done.1 = bf16[1,64,16,128]{3,2,0,1:T(8,128)(2,1)S(1)} async-done(((bf16[1,64,16,128]{3,2,0,1:T(8,128)(2,1)}), bf16[1,64,16,128]{3,2,0,1:T(8,128)(2,1)S(1)}, u32[]{:S(2)}, u32[]{:S(2)}) %all-to-all-start.1) | async-done | bytes 262176 | tf_op jit(solution)/shard_map/all_to_all | solution.py:71
  151.2 0.9 dynamic-slice_select_fusion
  152.1 4.2 %all_to_all.35 = bf16[2,1,64,16,128]{4,3,2,1,0:T(8,128)(2,1)S(1)} all-to-all(bf16[2,1,64,16,128]{4,3,2,1,0:T(8,128)(2,1)S(1)} %broadcast_in_dim.64), channel_id=1, replica_groups=mesh['dp'=64,'mp'=2] {'mp'}, dimensions={0} | all-to-all | bytes 1048576 | tf_op jit(solution)/shard_map/all_to_all | solution.py:19
  156.3 4.9 %all-to-all-start.4 = ((bf16[1,64,16,128]{3,2,0,1:T(8,128)(2,1)}), bf16[1,64,16,128]{3,2,0,1:T(8,128)(2,1)S(1)}, u32[]{:S(2)}, u32[]{:S(2)}) async-start(bf16[1,64,16,128]{3,2,0,1:T(8,128)(2,1)} %get-tuple-element.11), calls=%async_computation.4 | async-start | bytes 524288 | tf_op jit(solution)/shard_map/all_to_all | solution.py:88
  161.2 0.8 copy.38
  162.0 10.1 %all-to-all-done.4 = bf16[1,64,16,128]{3,2,0,1:T(8,128)(2,1)S(1)} async-done(((bf16[1,64,16,128]{3,2,0,1:T(8,128)(2,1)}), bf16[1,64,16,128]{3,2,0,1:T(8,128)(2,1)S(1)}, u32[]{:S(2)}, u32[]{:S(2)}) %all-to-all-start.4) | async-done | bytes 262176 | tf_op jit(solution)/shard_map/all_to_all | solution.py:88
  172.2 4.2 %all_to_all.36 = bf16[2,1,64,16,128]{4,3,2,1,0:T(8,128)(2,1)S(1)} all-to-all(bf16[2,1,64,16,128]{4,3,2,1,0:T(8,128)(2,1)S(1)} %broadcast_in_dim.68), channel_id=1, replica_groups=mesh['dp'=64,'mp'=2] {'mp'}, dimensions={0} | all-to-all | bytes 1048576 | tf_op jit(solution)/shard_map/all_to_all | solution.py:19
  176.3 1.1 copy_convert_fusion
  177.5 13.2 %scatter_custom_fusion = f32[4096,128]{1,0:T(8,128)} fusion(s32[2048]{0:T(1024)S(1)} %bitcast.53, f32[2048,128]{1,0:T(8,128)} %bitcast.47, f32[]{:T(128)} %constant.31.clone.1), kind=kCustom, calls=%fused_computation.27 | custom fusion | flops 262144 | bytes 2097664 | tf_op jit(solution)/shard_map/scatter-add | solution.py:113
  190.7 3.2 %multiply_subtract_fusion = f32[4096,128]{1,0:T(8,128)} fusion(f32[4096,128]{1,0:T(8,128)S(1)} %copy-done.2, f32[4096,128]{1,0:T(8,128)} %scatter_custom_fusion), kind=kLoop, calls=%fused_computation.22 | loop fusion | flops 1048576 | bytes 6291456 | tf_op jit(solution)/shard_map/sub | solution.py:115
  193.9 0.4 fusion.26
  194.4 4.6 %all_to_all.37 = f32[2,1024,128]{2,1,0:T(8,128)S(1)} all-to-all(f32[2,1024,128]{2,1,0:T(8,128)S(1)} %broadcast_in_dim.69), channel_id=1, replica_groups=mesh['dp'=64,'mp'=2] {'mp'}, dimensions={0} | all-to-all | bytes 2097152 | tf_op jit(solution)/shard_map/all_to_all | solution.py:19
  199.0 0.8 reduce_sum.28
  199.8 55.6 %all-reduce.3.cloned.1.call-done = (f32[1024,512]{1,0:T(8,128)}, f32[512,1024]{1,0:T(8,128)}, f32[1024,512]{1,0:T(8,128)}, f32[512,128]{1,0:T(8,128)}) async-done(((f32[1024,512]{1,0:T(8,128)}, f32[512,1024]{1,0:T(8,128)}, f32[1024,512]{1,0:T(8,128)}, f32[512,128]{1,0:T(8,128)}), (f32[1024,512]{1,0:T(8,128)}, f32[512,1024]{1,0:T(8,128)}, f32[1024,512]{1,0:T(8,128)}, ...) | async-done | bytes 6553616 | tf_op jit(solution)/shard_map/psum | solution.py:104
  255.4 3.2 %copy.49 = f32[1024,512]{1,0:T(8,128)} copy(f32[1024,512]{1,0:T(8,128)} %get-tuple-element.18) | data formatting | bytes 4194304
  258.7 1.3 copy.50
  260.0 1.0 copy-done.6
  261.0 1.3 copy.51
  262.3 0.7 copy.52
  (63 shorter events, 1.3 us)
Async XLA Ops:
  7.2 44.6 %copy-start = (bf16[1024,512]{1,0:T(8,128)(2,1)S(1)}, bf16[1024,512]{1,0:T(8,128)(2,1)}, u32[]{:S(2)}) copy-start(bf16[1024,512]{1,0:T(8,128)(2,1)} %param.21) | copy-start | bytes 3145732
  7.2 6.2 %copy-start.14 = (bf16[512,1024]{1,0:T(8,128)(2,1)S(1)}, bf16[512,1024]{1,0:T(8,128)(2,1)}, u32[]{:S(2)}) copy-start(bf16[512,1024]{1,0:T(8,128)(2,1)} %param.20) | copy-start | bytes 3145732
  7.2 34.6 %all-gather.5.cloned.1.call-start = ((), (), s32[]{:S(2)}) async-start(), calls=%async_computation.7 | async-start | bytes 12582912 | tf_op jit(solution)/shard_map/all_gather | solution.py:14
  12.0 1.3 copy-start.19
  16.6 65.0 %all-gather.7.cloned.1.call-start = ((), (), s32[]{:S(2)}) async-start(), calls=%async_computation.8 | async-start | bytes 12582912 | tf_op jit(solution)/shard_map/all_gather | solution.py:14
  51.8 1.6 copy-start.5
  51.8 1.6 copy-start.9
  51.8 1.6 copy-start.11
  53.4 4.4 %copy-start.3 = (bf16[1024,512]{1,0:T(8,128)(2,1)}, bf16[1024,512]{1,0:T(8,128)(2,1)S(1)}, u32[]{:S(2)}) copy-start(bf16[1024,512]{1,0:T(8,128)(2,1)S(1)} %get-tuple-element.13) | copy-start | bytes 3145732
  57.5 197.9 %all-reduce.3.cloned.1.call-start = ((), (), s32[]{:S(2)}) async-start(), calls=%async_computation.9 | async-start | bytes 13107200 | tf_op jit(solution)/shard_map/psum | solution.py:104
  88.2 5.1 %copy-start.20 = (f32[1024,512]{1,0:T(8,128)S(1)}, f32[1024,512]{1,0:T(8,128)}, u32[]{:S(2)}) copy-start(f32[1024,512]{1,0:T(8,128)} %copy-done.19) | copy-start | bytes 6291460
  93.3 2.7 copy-start.15
  93.3 2.7 copy-start.16
  93.3 2.7 copy-start.17
  93.3 2.7 copy-start.18
  104.1 0.7 copy-start.12
  104.1 27.2 %copy-start.2 = (f32[4096,128]{1,0:T(8,128)S(1)}, f32[4096,128]{1,0:T(8,128)}, u32[]{:S(2)}) copy-start(f32[4096,128]{1,0:T(8,128)} %param.15) | copy-start | bytes 6291460
  104.2 36.0 %copy-start.13 = (s32[1,64]{1,0:T(1,128)S(1)}, s32[1,64]{1,0:T(1,128)}, u32[]{:S(2)}) copy-start(s32[1,64]{1,0:T(1,128)} %param.13) | copy-start | bytes 772
  104.2 47.0 %copy-start.10 = (bf16[1,64,32,128]{3,2,1,0:T(8,128)(2,1)S(1)}, bf16[1,64,32,128]{3,2,1,0:T(8,128)(2,1)}, u32[]{:S(2)}) copy-start(bf16[1,64,32,128]{3,2,1,0:T(8,128)(2,1)} %param.14) | copy-start | bytes 1572868
  105.5 20.2 %all-to-all-start = ((s32[1,64,16]{2,0,1:T(1,128)}), s32[1,64,16]{2,0,1:T(1,128)S(1)}, u32[]{:S(2)}, u32[]{:S(2)}) async-start(s32[1,64,16]{2,0,1:T(1,128)} %copy.43), calls=%async_computation | async-start | bytes 65536 | tf_op jit(solution)/shard_map/all_to_all | solution.py:68
  126.5 8.6 %all-to-all-start.3 = ((s32[2,1,1024]{2,1,0:T(1,128)}), s32[2,1,1024]{2,1,0:T(1,128)S(1)}, u32[]{:S(2)}, u32[]{:S(2)}) async-start(s32[2,1,1024]{2,1,0:T(1,128)} %reshape.200), calls=%async_computation.3 | async-start | bytes 16384 | tf_op jit(solution)/shard_map/all_to_all | solution.py:19
  135.2 16.0 %all-to-all-start.1 = ((bf16[1,64,16,128]{3,2,0,1:T(8,128)(2,1)}), bf16[1,64,16,128]{3,2,0,1:T(8,128)(2,1)S(1)}, u32[]{:S(2)}, u32[]{:S(2)}) async-start(bf16[1,64,16,128]{3,2,0,1:T(8,128)(2,1)} %select_convert_fusion), calls=%async_computation.1 | async-start | bytes 524288 | tf_op jit(solution)/shard_map/all_to_all | solution.py:71
  156.3 15.8 %all-to-all-start.4 = ((bf16[1,64,16,128]{3,2,0,1:T(8,128)(2,1)}), bf16[1,64,16,128]{3,2,0,1:T(8,128)(2,1)S(1)}, u32[]{:S(2)}, u32[]{:S(2)}) async-start(bf16[1,64,16,128]{3,2,0,1:T(8,128)(2,1)} %get-tuple-element.11), calls=%async_computation.4 | async-start | bytes 524288 | tf_op jit(solution)/shard_map/all_to_all | solution.py:88
  190.7 3.2 %copy-start.4 = (bf16[1024,512]{1,0:T(8,128)(2,1)S(1)}, bf16[1024,512]{1,0:T(8,128)(2,1)}, u32[]{:S(2)}) copy-start(bf16[1024,512]{1,0:T(8,128)(2,1)} %copy-done.3) | copy-start | bytes 3145732
  255.4 3.2 %copy-start.7 = (f32[512,1024]{1,0:T(8,128)S(1)}, f32[512,1024]{1,0:T(8,128)}, u32[]{:S(2)}) copy-start(f32[512,1024]{1,0:T(8,128)} %get-tuple-element.19) | copy-start | bytes 6291460
  258.6 2.3 copy-start.6
  258.6 4.4 %copy-start.1 = (bf16[1024,512]{1,0:T(8,128)(2,1)S(1)}, bf16[1024,512]{1,0:T(8,128)(2,1)}, u32[]{:S(2)}) copy-start(bf16[1024,512]{1,0:T(8,128)(2,1)} %param.21) | copy-start | bytes 3145732
  261.0 1.3 copy-start.8
Sparse Core Ops, SparseCore 0:
  16.7 25.0 all-gather.4
  57.7 23.8 all-gather.6
  104.3 151.0 all-reduce.2
where the time goes:
time: 271 us; the launch traced here: 270 us
  waiting for transfers between devices  129 us (48%)
  other arithmetic  43.4 us (16%)
  matrix products  30.2 us (11%)
  starting transfers between devices  24 us (9%)
  local copies, waits for them, and re-layouts  16.5 us (6%)
  between operations  14.1 us (5%)
  blocking collectives  12.9 us (5%)
    psum x1, waiting for transfers between devices, local(): lax.psum((part_one, part_two, part_three, part_four), 'dp')  55.6 us
    all_gather x2, waiting for transfers between devices, over_pieces(): return lax.all_gather(array, axis).sum(0)  43.6 us
    reduce_sum x2, other arithmetic, over_pieces(): return lax.all_gather(array, axis).sum(0)  13.3 us
    scatter-add x1, other arithmetic, local(): delta = jnp.zeros_like(table).at[received.reshape(-1)].add(arrived.reshap...  13.2 us
    all_to_all x3, blocking collectives, from_everyone(): lax.all_to_all(jnp.broadcast_to(array[None], (size, *array.shape)), axis,...  12.9 us
    unnamed x50, local copies, waits for them, and re-layouts  11.2 us
    all_to_all x1, starting transfers between devices, local(): lax.all_to_all(mine, 'dp', split_axis=1, concat_axis=1, tiled=True)  10.4 us
    all_to_all x1, waiting for transfers between devices, local(): lax.all_to_all(own_cot, 'dp', split_axis=1, concat_axis=1, tiled=True)  10.1 us
  transfers between devices with their start and end apart: 7, of which 6 were waited for; matrix products, arithmetic and copies ran while one was open for 13% of the time, Pallas kernels for 0%

commit v1 on v0

v1 whole, which is shorter than its diff:
```python
import functools

import jax
import jax.numpy as jnp
from jax import lax
from jax.experimental import pallas as pl
from jax.experimental.pallas import tpu as pltpu
from jax.sharding import PartitionSpec as P

MESH = pl.DeviceIdType.MESH
learn_rate = 0.5
modulus = 1000003
RING = 4
PLANE = RING * RING
CHUNKS = RING * PLANE

STREAMS = (
    (0, 0, 2, 0),
    (0, 2, 1, 1),
    (0, 3, 1, 2),
    (1, 0, 1, 1),
    (2, 0, 2, 1),
    (2, 2, 1, 2),
    (2, 3, 1, 0),
    (3, 0, 2, 2),
    (3, 2, 1, 0),
    (3, 3, 1, 1),
)
BLOCKS = (4, 1, 4, 4)
ROWS = (16, 8, 16, 16)
TYPES = (jnp.bfloat16, jnp.float32, jnp.bfloat16, jnp.bfloat16)
HALF = PLANE // 2


class Place:
    def __init__(self, axis):
        me = lax.axis_index("dp")
        self.core = lax.axis_index("mp")
        strides = (1, RING, RING * RING)
        self.stride = strides[axis]
        self.others = (strides[(axis + 1) % 3], strides[(axis + 2) % 3])
        self.k = lax.rem(me // self.stride, RING)
        self.first = lax.rem(me // self.others[0], RING)
        self.second = lax.rem(me // self.others[1], RING)
        self.p = self.first * RING + self.second
        self.after = lax.rem(self.k + 1, RING)
        self.before = lax.rem(self.k + RING - 1, RING)
        self.opposite = lax.rem(self.k + 2, RING)
        self.right = me + (self.after - self.k) * self.stride
        self.left = me + (self.before - self.k) * self.stride

    def peer(self, p):
        return (
            self.k * self.stride
            + (p // RING) * self.others[0]
            + lax.rem(p, RING) * self.others[1]
        )


class Stream:
    def __init__(self, index, refs, place):
        self.grad, self.b0, self.nb, axis = STREAMS[index]
        self.place = place[axis]
        self.index = index
        g = self.grad
        blocks = pl.ds(self.b0, self.nb)
        self.own = refs["own"][g].at[blocks]
        self.other = refs["other"][g].at[blocks]
        self.arrive = refs["arrive"][g].at[blocks]
        self.total = refs["total"][g].at[blocks]
        self.out = refs["out"][g].at[blocks]
        self.near = refs["near"][g].at[blocks]
        self.side = refs["side"][g].at[blocks]
        self.part = refs["part"][g].at[blocks]
        self.fan = refs["fan"][g].at[blocks]
        self.final = refs["final"][g].at[blocks]
        self.send = refs["send"]
        self.recv = refs["recv"]
        self.dtype = TYPES[g]
        self.pending = []

    def sems(self, slot):
        return self.send.at[self.index, slot], self.recv.at[self.index, slot]

    def copy(self, src, dst, slot, device):
        s, r = self.sems(slot)
        return pltpu.make_async_remote_copy(
            src_ref=src, dst_ref=dst, send_sem=s, recv_sem=r,
            device_id=device, device_id_type=MESH,
        )

    def start(self, src, dst, slot, dp=None, mp=None):
        where = (
            lax.axis_index("dp") if dp is None else dp,
            self.place.core if mp is None else mp,
        )
        c = self.copy(src, dst, slot, where)
        c.start()
        self.pending.append(c)
        return c

    def swap(self):
        self.c_swap = self.start(self.other, self.arrive, 0, mp=1 - self.place.core)

    def chunk(self, ref, first, count):
        return ref.at[:, pl.ds(first, count)]

    def combine(self):
        self.c_swap.wait_recv()

        @pl.loop(0, CHUNKS // 2)
        def _(i):
            rows = pl.ds(i * 2, 2)
            self.total[:, rows] = (
                self.own[:, rows].astype(jnp.float32)
                + self.arrive[:, rows].astype(jnp.float32)
            ).astype(self.dtype)

        q = self.place
        base = q.opposite * PLANE
        self.c_na = self.start(
            self.chunk(self.total, base, HALF), self.chunk(self.near, 0, HALF), 1, dp=q.right
        )
        self.c_nb = self.start(
            self.chunk(self.total, base + HALF, HALF), self.chunk(self.near, HALF, HALF), 2, dp=q.left
        )
        self.c_sa = self.start(
            self.chunk(self.total, q.after * PLANE + HALF, HALF),
            self.chunk(self.side, HALF, HALF), 3, dp=q.right,
        )
        self.c_sb = self.start(
            self.chunk(self.total, q.before * PLANE, HALF),
            self.chunk(self.side, PLANE, HALF), 4, dp=q.left,
        )

    def relay(self):
        q = self.place
        for copy, place, slot_from, slot, target, side in (
            (self.c_na, q.after * PLANE, 0, 5, q.right, 0),
            (self.c_nb, q.before * PLANE + HALF, HALF, 6, q.left, PLANE + HALF),
        ):
            copy.wait_recv()

            @pl.loop(0, HALF)
            def _(i, place=place, slot_from=slot_from):
                rows = pl.ds(place + i, 1)
                self.total[:, rows] = (
                    self.total[:, rows].astype(jnp.float32)
                    + self.near[:, pl.ds(slot_from + i, 1)].astype(jnp.float32)
                ).astype(self.dtype)

            c = self.start(
                self.chunk(self.total, place, HALF), self.chunk(self.side, side, HALF), slot, dp=target
            )
            if slot == 5:
                self.c_ra = c
            else:
                self.c_rb = c

    def spread(self):
        q = self.place
        for c in (self.c_sa, self.c_sb, self.c_ra, self.c_rb):
            c.wait_recv()

        @pl.loop(0, PLANE)
        def _(i):
            self.part[:, pl.ds(i, 1)] = (
                self.total[:, pl.ds(q.k * PLANE + i, 1)].astype(jnp.float32)
                + self.side[:, pl.ds(i, 1)].astype(jnp.float32)
                + self.side[:, pl.ds(PLANE + i, 1)].astype(jnp.float32)
            ).astype(self.dtype)

        @pl.loop(1, PLANE)
        def _(j):
            p = lax.rem(q.p + j, PLANE)
            self.copy(
                self.chunk(self.part, p, 1), self.chunk(self.fan, j - 1, 1), 7,
                (q.peer(p), q.core),
            ).start()

    def wait_fan(self, slot, ref, recv):
        s, r = self.sems(slot)
        fifteen = self.chunk(ref, 0, PLANE - 1)
        pltpu.make_async_copy(fifteen, fifteen, r if recv else s).wait()

    def finish(self):
        q = self.place
        self.wait_fan(7, self.fan, True)
        acc = self.part[:, pl.ds(q.p, 1)].astype(jnp.float32)
        for i in range(PLANE - 1):
            acc = acc + self.fan[:, pl.ds(i, 1)].astype(jnp.float32)
        acc = acc.astype(self.dtype)
        self.final[...] = acc
        here = q.k * PLANE + q.p
        self.out[:, pl.ds(here, 1)] = acc

        @pl.loop(1, PLANE)
        def _(j):
            p = lax.rem(q.p + j, PLANE)
            self.copy(
                self.final, self.chunk(self.out, here, 1), 8, (q.peer(p), q.core)
            ).start()

    def share(self):
        q = self.place
        self.wait_fan(8, self.out, True)
        low = self.chunk(self.out, q.k * PLANE, HALF)
        high = self.chunk(self.out, q.k * PLANE + HALF, HALF)
        self.c_gl = self.start(low, low, 9, dp=q.right)
        self.c_gh = self.start(high, high, 10, dp=q.left)
        self.c_hh = self.start(high, high, 11, dp=q.right)
        self.c_hl = self.start(low, low, 12, dp=q.left)

    def forward(self):
        q = self.place
        self.c_gl.wait_recv()
        low = self.chunk(self.out, q.before * PLANE, HALF)
        self.c_fl = self.start(low, low, 13, dp=q.right)
        self.c_gh.wait_recv()
        high = self.chunk(self.out, q.after * PLANE + HALF, HALF)
        self.c_fh = self.start(high, high, 14, dp=q.left)

    def close(self):
        for c in (self.c_hh, self.c_hl, self.c_fl, self.c_fh):
            c.wait_recv()

    def drain(self):
        for c in self.pending:
            c.wait_send()
        self.wait_fan(7, self.fan, False)
        self.wait_fan(8, self.out, False)


SLOTS = 15


def greet(places):
    barrier = pltpu.get_barrier_semaphore()
    me = lax.axis_index("dp")
    core = places[0].core
    pl.semaphore_signal(barrier, inc=1, device_id=(me, 1 - core), device_id_type=MESH)
    for q in places:
        @pl.loop(1, PLANE)
        def _(j, q=q):
            pl.semaphore_signal(
                barrier, inc=1,
                device_id=(q.peer(lax.rem(q.p + j, PLANE)), core), device_id_type=MESH,
            )
    pl.semaphore_wait(barrier, 1 + 3 * (PLANE - 1))


def reduce_kernel(*args):
    own, other, out = args[0:4], args[4:8], args[8:12]
    rest = args[12:]
    names = ("arrive", "total", "near", "side", "part", "fan", "final")
    refs = {name: rest[4 * i : 4 * i + 4] for i, name in enumerate(names)}
    refs.update(own=own, other=other, out=out)
    refs["send"], refs["recv"] = rest[4 * len(names) :]
    places = [Place(a) for a in range(3)]
    greet(places)
    streams = [Stream(i, refs, places) for i in range(len(STREAMS))]
    for s in streams:
        s.swap()
    for step in ("combine", "relay", "spread", "finish", "share", "forward", "close", "drain"):
        for s in streams:
            getattr(s, step)()


def shapes(count):
    return [
        pltpu.VMEM((BLOCKS[g], count, ROWS[g], 128), TYPES[g]) for g in range(4)
    ]


def reduce_all(own, other):
    vmem = pl.BlockSpec(memory_space=pltpu.VMEM)
    return pl.pallas_call(
        reduce_kernel,
        out_shape=[
            jax.ShapeDtypeStruct((BLOCKS[g], CHUNKS, ROWS[g], 128), TYPES[g]) for g in range(4)
        ],
        in_specs=[vmem] * 8,
        out_specs=[vmem] * 4,
        scratch_shapes=(
            shapes(CHUNKS)
            + shapes(CHUNKS)
            + shapes(PLANE)
            + shapes(2 * PLANE)
            + shapes(PLANE)
            + shapes(PLANE - 1)
            + shapes(1)
            + [
                pltpu.SemaphoreType.DMA((len(STREAMS), SLOTS)),
                pltpu.SemaphoreType.DMA((len(STREAMS), SLOTS)),
            ]
        ),
        compiler_params=pltpu.CompilerParams(
            collective_id=0, has_side_effects=True, vmem_limit_bytes=60 * 1024 * 1024
        ),
        name="reduce_all",
    )(*own, *other)


def features_of(ids, hash_mult, hash_add):
    hashed = jnp.remainder(ids[:, None] * hash_mult[None, :] + hash_add[None, :], modulus)
    return (hashed.astype(jnp.float32) * (2.0 / 1000002.0) - 1.0).astype(jnp.bfloat16)


def silu_grad(value):
    sig = jax.nn.sigmoid(value)
    return sig * (1.0 + value * (1.0 - sig))


def from_everyone(array, axis):
    size = lax.axis_size(axis)
    return lax.all_to_all(
        jnp.broadcast_to(array[None], (size, *array.shape)), axis, 0, 0, tiled=True
    )


def in_order(tiles, dim):
    dims = list(tiles.shape[1:])
    dims[dim] *= tiles.shape[0]
    return jnp.moveaxis(tiles, 0, dim).reshape(dims)


def gather_directly(array, axis, dim):
    return in_order(from_everyone(array, axis), dim)


def tall(g):
    return g.reshape(CHUNKS, 16, 4, 128).transpose(2, 0, 1, 3).astype(jnp.bfloat16)


def from_tall(t):
    return t.astype(jnp.float32).transpose(1, 2, 0, 3).reshape(1024, 512)


def wide(g):
    return g.reshape(512, 4, 2, 128).transpose(1, 2, 0, 3).reshape(4, CHUNKS, 16, 128).astype(jnp.bfloat16)


def from_wide(t):
    return t.astype(jnp.float32).reshape(4, 2, 512, 128).transpose(2, 0, 1, 3).reshape(512, 1024)


def local(
    hot_rows, hot_count, hot_cot, table, cold_ids, hash_mult, hash_add,
    layer_one, layer_two, layer_three, layer_four, cold_cot,
):
    width = table.shape[1]
    core = lax.axis_index("mp")
    span = hot_rows.shape[2] // 2
    begin = core * span
    f32 = jnp.float32

    def dot(a, b):
        return jnp.dot(a, b, preferred_element_type=f32)

    def partner(x):
        return lax.ppermute(x, "mp", [(0, 1), (1, 0)])

    w1, w2, w3, w4 = layer_one, layer_two, layer_three, layer_four
    v1, v2, v3, v4 = partner(w1), partner(w2), partner(w3), partner(w4)
    tokens = cold_ids.shape[0] // 2
    ids = lax.dynamic_slice_in_dim(cold_ids, core * tokens, tokens, 0)
    cot = lax.dynamic_slice_in_dim(cold_cot, core * tokens, tokens, 0)
    feats = features_of(ids, hash_mult, hash_add)

    def act(v):
        return jax.nn.silu(v).astype(jnp.bfloat16)

    p1, q1 = dot(feats, w1), dot(feats, v1)
    a1, c1 = act(p1), act(q1)
    p2 = dot(a1, w2) + dot(c1, v2)
    a2 = act(p2)
    p3, q3 = dot(a2, w3), dot(a2, v3)
    a3, c3 = act(p3), act(q3)
    emb = (dot(a3, w4) + dot(c3, v4)).astype(jnp.bfloat16)
    emb_other = partner(emb)
    first = jnp.where(core == 0, emb, emb_other)
    last = jnp.where(core == 0, emb_other, emb)
    cold_emb = jnp.concatenate([first, last], 0)

    def back(v, pre):
        return (v * silu_grad(pre)).astype(jnp.bfloat16)

    b3, d3 = back(dot(cot, w4.T), p3), back(dot(cot, v4.T), q3)
    g4, h4 = dot(a3.T, cot), dot(c3.T, cot)
    b2 = back(dot(b3, w3.T) + dot(d3, v3.T), p2)
    g3, h3 = dot(a2.T, b3), dot(a2.T, d3)
    b1, d1 = back(dot(b2, w2.T), p1), back(dot(b2, v2.T), q1)
    g2, h2 = dot(a1.T, b2), dot(c1.T, b2)
    g1, h1 = dot(feats.T, b1), dot(feats.T, d1)

    own = [tall(g3), g4.reshape(1, CHUNKS, 8, 128), wide(g2), tall(g1)]
    other = [tall(h3), h4.reshape(1, CHUNKS, 8, 128), wide(h2), tall(h1)]
    o3, o4, o2, o1 = reduce_all(own, other)
    factor = float(cold_ids.shape[0] * lax.axis_size("dp")) ** (-0.5)
    grad_one = from_tall(o1) * factor
    grad_two = from_wide(o2) * factor
    grad_three = from_tall(o3) * factor
    grad_four = o4.reshape(512, 128) * factor

    mine = lax.dynamic_slice_in_dim(hot_rows, begin, span, 2)
    received = lax.all_to_all(mine, "dp", split_axis=1, concat_axis=1, tiled=True)
    fetched = jnp.take(table, received.reshape(-1), axis=0).astype(jnp.bfloat16)
    fetched = fetched.reshape(received.shape + (width,))
    returned = lax.all_to_all(fetched, "dp", split_axis=1, concat_axis=1, tiled=True)
    slot_index = begin + jnp.arange(span, dtype=jnp.int32)
    used = slot_index[None, None, :] < hot_count[:, :, None]
    own_emb = jnp.where(used[..., None], returned, jnp.zeros_like(returned))
    own_cot = lax.dynamic_slice_in_dim(hot_cot, begin, span, 2)
    own_cot = jnp.where(used[..., None], own_cot, jnp.zeros_like(own_cot))
    arrived = lax.all_to_all(own_cot, "dp", split_axis=1, concat_axis=1, tiled=True)
    arrived = gather_directly(arrived, "mp", 2)
    received = gather_directly(received, "mp", 2)
    hot_emb = gather_directly(own_emb, "mp", 2)
    delta = (
        jnp.zeros_like(table)
        .at[received.reshape(-1)]
        .add(arrived.reshape(-1, width).astype(jnp.float32))
    )
    new_table = table - learn_rate * delta
    return (hot_emb, new_table, cold_emb, grad_one, grad_two, grad_three, grad_four)


def solution(mesh):
    in_specs = (
        P("dp", None, None),
        P("dp", None),
        P("dp", None, None, None),
        P("dp", None),
        P("dp"),
        P(),
        P(),
        P(None, "mp"),
        P("mp", None),
        P(None, "mp"),
        P("mp", None),
        P("dp", None),
    )
    out_specs = (
        P("dp", None, None, None),
        P("dp", None),
        P("dp", None),
        P(None, "mp"),
        P("mp", None),
        P(None, "mp"),
        P("mp", None),
    )
    return jax.shard_map(local, mesh=mesh, in_specs=in_specs, out_specs=out_specs, check_vma=False)
```

time: 271 us -> 224 us (0.83); the launches traced: 270 us -> 220 us
  waiting for transfers between devices: 129 us -> 23.9 us
  Pallas kernels: 0 us -> 49.3 us
  matrix products: 30.2 us -> 50.1 us
  other arithmetic: 43.4 us -> 24.4 us
  local copies, waits for them, and re-layouts: 16.5 us -> 34.7 us
  between operations: 14.1 us -> 1.32 us
  blocking collectives: 12.9 us -> 8.31 us
  starting transfers between devices: 24 us -> 27.6 us
    psum x1 -> x0, waiting for transfers between devices: 55.6 us -> none  [local(): lax.psum((part_one, part_two, part_three, part_four), 'dp')]
    pallas_call x0 -> x1, Pallas kernels: none -> 49.3 us  [reduce_all(): pl.pallas_call(reduce_kernel, out_shape=[jax.ShapeDtypeStruct((BLOCKS[g],...]
    all_gather x2 -> x0, waiting for transfers between devices: 43.6 us -> none  [over_pieces(): return lax.all_gather(array, axis).sum(0)]
    dot_general x10 -> x20, matrix products: 30.2 us -> 50.1 us  [dot(): return jnp.dot(a, b, preferred_element_type=f32)]
    convert_element_type x0 -> x12, local copies, waits for them, and re-layouts: none -> 14.5 us  [the longest x8 8.75 us: tall(): g.reshape(CHUNKS, 16, 4, 128).transpose(2, 0, 1, 3).astype(jnp.bfloat16)]
    reduce_sum x3 -> x0, other arithmetic: 14.1 us -> none  [the longest x2 13.3 us: over_pieces(): return lax.all_gather(array, axis).sum(0)]
    convert_element_type x2 -> x0, other arithmetic: 8.34 us -> none  [the longest x1 5.05 us: local(): back_two = (back_sum * silu_grad(pre_two)).astype(jnp.bfloat16)]
    mul x0 -> x4, local copies, waits for them, and re-layouts: none -> 7 us  [the longest x2 4.3 us: local(): grad_two = from_wide(o2) * factor]
  transfers between devices with their start and end apart: 7 -> 9, of which waited for: 6 -> 4; matrix products, arithmetic and copies ran while one was open for 13% -> 20% of each run, Pallas kernels for 0% -> 0%
where the time goes in v1:
time: 224 us; the launch traced here: 220 us
  matrix products  50.1 us (22%)
  Pallas kernels  49.3 us (22%)
  local copies, waits for them, and re-layouts  34.7 us (15%)
  starting transfers between devices  27.6 us (12%)
  other arithmetic  24.4 us (11%)
  waiting for transfers between devices  23.9 us (11%)
  blocking collectives  8.31 us (4%)
    dot_general x20, matrix products, dot(): return jnp.dot(a, b, preferred_element_type=f32)  50.1 us
    pallas_call x1, Pallas kernels, reduce_all(): pl.pallas_call(reduce_kernel, out_shape=[jax.ShapeDtypeStruct((BLOCKS[g],...  49.3 us
    scatter-add x1, other arithmetic, local(): delta = jnp.zeros_like(table).at[received.reshape(-1)].add(arrived.reshap...  13.1 us
    all_to_all x1, starting transfers between devices, local(): lax.all_to_all(mine, 'dp', split_axis=1, concat_axis=1, tiled=True)  11.5 us
    all_to_all x1, waiting for transfers between devices, local(): lax.all_to_all(own_cot, 'dp', split_axis=1, concat_axis=1, tiled=True)  10.1 us
    all_to_all x1, waiting for transfers between devices, local(): lax.all_to_all(fetched, 'dp', split_axis=1, concat_axis=1, tiled=True)  9.64 us
    convert_element_type x8, local copies, waits for them, and re-layouts, tall(): g.reshape(CHUNKS, 16, 4, 128).transpose(2, 0, 1, 3).astype(jnp.bfloat16)  8.75 us
    all_to_all x2, blocking collectives, from_everyone(): lax.all_to_all(jnp.broadcast_to(array[None], (size, *array.shape)), axis,...  8.31 us
  transfers between devices with their start and end apart: 9, of which 4 were waited for; matrix products, arithmetic and copies ran while one was open for 20% of the time, Pallas kernels for 0%

profile of v1, /device:TPU:0, one launch (start us, length us, event | category | flops | bytes accessed | tf_op | source)
XLA Modules:
  0.0 219.6 jit_solution(2975617034320198576)
XLA Ops:
  3.1 11.5 %all-to-all-start = ((s32[1,64,16]{2,0,1:T(1,128)}), s32[1,64,16]{2,0,1:T(1,128)S(1)}, u32[]{:S(2)}, u32[]{:S(2)}) async-start(s32[1,64,16]{2,0,1:T(1,128)} %copy.66), calls=%async_computation | async-start | bytes 65536 | tf_op jit(solution)/shard_map/all_to_all | solution.py:406
  15.5 3.1 %fusion.24 = f32[512,512]{1,0:T(8,128)S(1)} fusion(bf16[1024,512]{1,0:T(8,128)(2,1)} %param.19, s32[1024]{0:T(1024)} %param.18, s32[1024]{0:T(1024)} %param.17, s32[512]{0:T(512)S(1)} %dynamic_slice.14), kind=kOutput, calls=%fused_computation.60 | convolution fusion | flops 543162368 | bytes 2107392 | tf_op jit(solution)/shard_map/dot_general | solution.py:358
  18.6 2.0 fusion.56
  20.7 3.5 %all-to-all-done = s32[1,64,16]{2,0,1:T(1,128)S(1)} async-done(((s32[1,64,16]{2,0,1:T(1,128)}), s32[1,64,16]{2,0,1:T(1,128)S(1)}, u32[]{:S(2)}, u32[]{:S(2)}) %all-to-all-start) | async-done | bytes 4128 | tf_op jit(solution)/shard_map/all_to_all | solution.py:406
  26.3 3.2 %all-to-all-start.3 = ((s32[2,1,1024]{2,1,0:T(1,128)}), s32[2,1,1024]{2,1,0:T(1,128)S(1)}, u32[]{:S(2)}, u32[]{:S(2)}) async-start(s32[2,1,1024]{2,1,0:T(1,128)} %reshape.236), calls=%async_computation.3 | async-start | bytes 16384 | tf_op jit(solution)/shard_map/all_to_all | solution.py:316
  29.6 2.9 %gather_fusion = bf16[1024,128]{1,0:T(8,128)(2,1)S(1)} fusion(f32[4096,128]{1,0:T(8,128)S(1)} %copy-done.1, s32[1024]{0:T(1024)S(1)} %broadcast_clamp_fusion), kind=kCustom, calls=%fused_computation | custom fusion | bytes 528384 | tf_op jit(solution)/shard_map/jit(_take)/gather | solution.py:407
  33.4 6.8 %all-to-all-start.1 = ((bf16[1,64,16,128]{3,2,0,1:T(8,128)(2,1)}), bf16[1,64,16,128]{3,2,0,1:T(8,128)(2,1)S(1)}, u32[]{:S(2)}, u32[]{:S(2)}) async-start(bf16[1,64,16,128]{3,2,0,1:T(8,128)(2,1)} %select_convert_fusion), calls=%async_computation.1 | async-start | bytes 524288 | tf_op jit(solution)/shard_map/all_to_all | solution.py:409
  41.8 9.6 %all-to-all-done.1 = bf16[1,64,16,128]{3,2,0,1:T(8,128)(2,1)S(1)} async-done(((bf16[1,64,16,128]{3,2,0,1:T(8,128)(2,1)}), bf16[1,64,16,128]{3,2,0,1:T(8,128)(2,1)S(1)}, u32[]{:S(2)}, u32[]{:S(2)}) %all-to-all-start.1) | async-done | bytes 262176 | tf_op jit(solution)/shard_map/all_to_all | solution.py:409
  51.4 0.9 dynamic-slice_select_fusion
  52.4 4.2 %all_to_all.30 = bf16[2,1,64,16,128]{4,3,2,1,0:T(8,128)(2,1)S(1)} all-to-all(bf16[2,1,64,16,128]{4,3,2,1,0:T(8,128)(2,1)S(1)} %broadcast_in_dim.58), channel_id=1, replica_groups=mesh['dp'=64,'mp'=2] {'mp'}, dimensions={0} | all-to-all | bytes 1048576 | tf_op jit(solution)/shard_map/all_to_all | solution.py:316
  56.6 4.9 %all-to-all-start.4 = ((bf16[1,64,16,128]{3,2,0,1:T(8,128)(2,1)}), bf16[1,64,16,128]{3,2,0,1:T(8,128)(2,1)S(1)}, u32[]{:S(2)}, u32[]{:S(2)}) async-start(bf16[1,64,16,128]{3,2,0,1:T(8,128)(2,1)} %get-tuple-element.17), calls=%async_computation.4 | async-start | bytes 524288 | tf_op jit(solution)/shard_map/all_to_all | solution.py:415
  62.3 10.1 %all-to-all-done.4 = bf16[1,64,16,128]{3,2,0,1:T(8,128)(2,1)S(1)} async-done(((bf16[1,64,16,128]{3,2,0,1:T(8,128)(2,1)}), bf16[1,64,16,128]{3,2,0,1:T(8,128)(2,1)S(1)}, u32[]{:S(2)}, u32[]{:S(2)}) %all-to-all-start.4) | async-done | bytes 262176 | tf_op jit(solution)/shard_map/all_to_all | solution.py:415
  72.5 4.2 %all_to_all.31 = bf16[2,1,64,16,128]{4,3,2,1,0:T(8,128)(2,1)S(1)} all-to-all(bf16[2,1,64,16,128]{4,3,2,1,0:T(8,128)(2,1)S(1)} %broadcast_in_dim.62), channel_id=1, replica_groups=mesh['dp'=64,'mp'=2] {'mp'}, dimensions={0} | all-to-all | bytes 1048576 | tf_op jit(solution)/shard_map/all_to_all | solution.py:316
  76.7 13.1 %scatter_custom_fusion = f32[4096,128]{1,0:T(8,128)} fusion(s32[2048]{0:T(1024)S(1)} %bitcast.114, f32[2048,128]{1,0:T(8,128)S(1)} %bitcast.108, f32[]{:T(128)} %constant.32.clone.1), kind=kCustom, calls=%fused_computation.61 | custom fusion | flops 262144 | bytes 2097156 | tf_op jit(solution)/shard_map/scatter-add | solution.py:422
  89.9 3.1 %multiply_subtract_fusion = f32[4096,128]{1,0:T(8,128)} fusion(f32[4096,128]{1,0:T(8,128)S(1)} %copy-done.1, f32[4096,128]{1,0:T(8,128)} %scatter_custom_fusion), kind=kLoop, calls=%fused_computation.18 | loop fusion | flops 1048576 | bytes 6291456 | tf_op jit(solution)/shard_map/sub | solution.py:424
  93.0 3.2 %fusion.22 = f32[512,512]{1,0:T(8,128)S(1)} fusion(bf16[1024,512]{1,0:T(8,128)(2,1)} %collective-permute-done, s32[1024]{0:T(1024)S(1)} %copy-done.10, s32[1024]{0:T(1024)S(1)} %copy-done.11, s32[512]{0:T(512)S(1)} %dynamic_slice.14), kind=kOutput, calls=%fused_computation.59 | convolution fusion | flops 543162368 | bytes 2107392 | tf_op jit(solution)/shard_map/dot_general | solution.py:358
  96.2 2.7 %multiply_convert_fusion.1 = (bf16[512,1024]{1,0:T(8,128)(2,1)S(1)}, f32[512,1024]{1,0:T(8,128)S(1)}) fusion(f32[512,1024]{1,0:T(8,128)S(1)} %copy-done.16, bf16[512,1024]{1,0:T(8,128)(2,1)} %collective-permute-done.1, f32[512,512]{1,0:T(8,128)S(1)} %fusion.22), kind=kOutput, calls=%fused_computation.13 | convolution fusion | flops 541327360 | bytes 7340032 | tf_op jit(solution)/shard_map/dot_general | solution.py:358
  100.5 2.1 multiply_convert_fusion.2
  104.6 2.3 %multiply_convert_fusion = bf16[512,1024]{1,0:T(8,128)(2,1)S(1)} fusion(f32[512,1024]{1,0:T(8,128)S(1)} %get-tuple-element.20, f32[512,1024]{1,0:T(8,128)S(1)} %fusion.58, bf16[512,512]{1,0:T(8,128)(2,1)S(1)} %fusion.8, bf16[1024,512]{1,0:T(8,128)(2,1)} %collective-permute-done.2), kind=kOutput, calls=%fused_computation.12 | convolution fusion | flops 542113792 | bytes 6815744 | tf_op jit(solution)/shard_map/dot_general | solution.py:358
  107.0 1.0 copy-done.19
  107.9 1.8 convolution_convert_fusion.1
  109.8 5.2 %convolution_convert_fusion.3 = bf16[1024,512]{1,0:T(8,128)(2,1)} fusion(bf16[512,1024]{1,0:T(8,128)(2,1)} %copy-done.19, bf16[512,1024]{1,0:T(8,128)(2,1)S(1)} %copy-done.9, f32[512,512]{1,0:T(8,128)} %copy-done.17, s32[1024]{0:T(1024)S(1)} %copy-done.10, s32[1024]{0:T(1024)S(1)} %copy-done.11, s32[512]{0:T(512)S(1)} %dynamic_slice.14), kind=kOutput, calls=%fused_computation.24 | convolution fusion | flops 1082916864 | bytes 4204544 | tf_op jit(solution)/shard_map/dot_general | solution.py:358
  114.9 3.4 %convolution_convert_fusion.4 = bf16[512,1024]{1,0:T(8,128)(2,1)} fusion(bf16[512,1024]{1,0:T(8,128)(2,1)} %copy-done.19, f32[512,512]{1,0:T(8,128)} %copy-done.17), kind=kOutput, calls=%fused_computation.25 | convolution fusion | flops 538705920 | bytes 3145728 | tf_op jit(solution)/shard_map/dot_general | solution.py:358
  118.4 1.7 convolution_convert_fusion.2
  120.8 11.4 %convolution_bitcast_fusion.1.args_1_ = f32[1,64,8,128]{3,2,1,0:T(8,128)} fusion(bf16[512,512]{1,0:T(8,128)(2,1)S(1)} %get-tuple-element.21, bf16[1024,128]{1,0:T(8,128)(2,1)S(1)} %copy-done, s32[]{:T(128)S(6)} %select_n.80), kind=kOutput, calls=%fused_computation.36 | convolution fusion | flops 67108864 | bytes 917508 | tf_op jit(solution)/shard_map/dot_general | solution.py:358
  132.2 1.0 fusion.57
  133.2 5.5 %convolution_convert_fusion = bf16[1024,512]{1,0:T(8,128)(2,1)} fusion(bf16[512,1024]{1,0:T(8,128)(2,1)} %copy-done.19, bf16[512,1024]{1,0:T(8,128)(2,1)} %collective-permute-done.1, f32[512,512]{1,0:T(8,128)} %copy-done.18, s32[1024]{0:T(1024)S(1)} %copy-done.10, s32[1024]{0:T(1024)S(1)} %copy-done.11, s32[512]{0:T(512)S(1)} %dynamic_slice.14), kind=kOutput, calls=%fused_computation.21 | convolution fusion | flops 1082916864 | bytes 4204544 | tf_op jit(solution)/shard_map/dot_general | solution.py:358
  138.7 1.3 convert_element_type.148
  140.1 1.1 copy.78
  141.2 1.8 convert_element_type.143
  143.0 1.1 copy.61
  144.1 1.3 convert_element_type.137
  145.4 1.1 copy.80
  146.5 1.8 convert_element_type.132
  148.3 1.1 copy.58
  149.4 1.3 convert_element_type.140
  150.8 1.1 copy.79
  152.2 1.1 copy.81
  153.3 1.1 convolution_bitcast_fusion.args_5_
  154.3 49.3 %reduce_all.1 = (bf16[4,64,16,128]{3,2,1,0:T(8,128)(2,1)}, f32[1,64,8,128]{3,2,1,0:T(8,128)}, bf16[4,64,16,128]{3,2,1,0:T(8,128)(2,1)}, bf16[4,64,16,128]{3,2,1,0:T(8,128)(2,1)}) custom-call(bf16[4,64,16,128]{3,2,1,0:T(8,128)(2,1)} %bitcast.103, f32[1,64,8,128]{3,2,1,0:T(8,128)} %convolution_bitcast_fusion.1.args_1_, bf16[4,64,16,128]{3,2,1,0:T(8,128)(2,1)} %bitcast.101, ...), custom_call_target="tpu_custom_call" | custom-call | tf_op jit(solution)/shard_map/reduce_all/pallas_call | solution.py:277
  203.7 1.9 multiply_bitcast_fusion
  205.5 1.4 copy.65
  206.9 1.5 copy.76
  208.4 1.6 copy.64
  210.0 2.7 %mul.169 = f32[512,1024]{1,0:T(8,128)} reshape(f32[512,4,2,128]{3,2,1,0:T(2,128)S(1)} %copy.64) | data formatting | bytes 4194304 | tf_op jit(solution)/shard_map/mul | solution.py:401
  212.7 1.4 multiply_bitcast_fusion.1
  214.1 1.4 copy.63
  215.5 1.5 copy.77
  (86 shorter events, 16.1 us)
Async XLA Ops:
  0.6 99.2 %copy-start = (bf16[1024,128]{1,0:T(8,128)(2,1)S(1)}, bf16[1024,128]{1,0:T(8,128)(2,1)}, u32[]{:S(2)}) copy-start(bf16[1024,128]{1,0:T(8,128)(2,1)} %param.23) | copy-start | bytes 786436
  0.6 92.4 %collective-permute-start = (bf16[1024,512]{1,0:T(8,128)(2,1)}, bf16[1024,512]{1,0:T(8,128)(2,1)}, u32[]{:S(2)}, u32[]{:S(2)}) collective-permute-start(bf16[1024,512]{1,0:T(8,128)(2,1)} %param.19), channel_id=1, source_target_pairs={{0,1},{1,0},{2,3},{3,2},{4,5},{5,4},{6,7},{7,6},{8,9},{9,8},{10,11... | collective-permute-start | bytes 3145736 | tf_op jit(solution)/shard_map/ppermute | solution.py:361
  0.7 95.4 %collective-permute-start.1 = (bf16[512,1024]{1,0:T(8,128)(2,1)}, bf16[512,1024]{1,0:T(8,128)(2,1)}, u32[]{:S(2)}, u32[]{:S(2)}) collective-permute-start(bf16[512,1024]{1,0:T(8,128)(2,1)} %param.20), channel_id=1, source_target_pairs={{0,1},{1,0},{2,3},{3,2},{4,5},{5,4},{6,7},{7,6},{8,9},{9,8},{10,11... | collective-permute-start | bytes 3145736 | tf_op jit(solution)/shard_map/ppermute | solution.py:361
  1.2 99.2 %collective-permute-start.2 = (bf16[1024,512]{1,0:T(8,128)(2,1)}, bf16[1024,512]{1,0:T(8,128)(2,1)}, u32[]{:S(2)}, u32[]{:S(2)}) collective-permute-start(bf16[1024,512]{1,0:T(8,128)(2,1)} %param.21), channel_id=1, source_target_pairs={{0,1},{1,0},{2,3},{3,2},{4,5},{5,4},{6,7},{7,6},{8,9},{9,8},{10,11... | collective-permute-start | bytes 3145736 | tf_op jit(solution)/shard_map/ppermute | solution.py:361
  1.3 102.0 %collective-permute-start.3 = (bf16[512,128]{1,0:T(8,128)(2,1)}, bf16[512,128]{1,0:T(8,128)(2,1)S(1)}, u32[]{:S(2)}, u32[]{:S(2)}) collective-permute-start(bf16[512,128]{1,0:T(8,128)(2,1)} %param.22), channel_id=1, source_target_pairs={{0,1},{1,0},{2,3},{3,2},{4,5},{5,4},{6,7},{7,6},{8,9},{9,8},{10,11... | collective-permute-start | bytes 393224 | tf_op jit(solution)/shard_map/ppermute | solution.py:361
  3.1 21.0 %all-to-all-start = ((s32[1,64,16]{2,0,1:T(1,128)}), s32[1,64,16]{2,0,1:T(1,128)S(1)}, u32[]{:S(2)}, u32[]{:S(2)}) async-start(s32[1,64,16]{2,0,1:T(1,128)} %copy.66), calls=%async_computation | async-start | bytes 65536 | tf_op jit(solution)/shard_map/all_to_all | solution.py:406
  15.4 3.1 %copy-start.8 = (bf16[512,1024]{1,0:T(8,128)(2,1)S(1)}, bf16[512,1024]{1,0:T(8,128)(2,1)}, u32[]{:S(2)}) copy-start(bf16[512,1024]{1,0:T(8,128)(2,1)} %param.20) | copy-start | bytes 3145732
  18.6 2.1 copy-start.17
  18.6 11.0 %copy-start.1 = (f32[4096,128]{1,0:T(8,128)S(1)}, f32[4096,128]{1,0:T(8,128)}, u32[]{:S(2)}) copy-start(f32[4096,128]{1,0:T(8,128)} %param.15) | copy-start | bytes 6291460
  20.6 19.5 %copy-start.7 = (s32[1,64]{1,0:T(1,128)S(1)}, s32[1,64]{1,0:T(1,128)}, u32[]{:S(2)}) copy-start(s32[1,64]{1,0:T(1,128)} %param.13) | copy-start | bytes 772
  20.6 30.8 %copy-start.6 = (bf16[1,64,32,128]{3,2,1,0:T(8,128)(2,1)S(1)}, bf16[1,64,32,128]{3,2,1,0:T(8,128)(2,1)}, u32[]{:S(2)}) copy-start(bf16[1,64,32,128]{3,2,1,0:T(8,128)(2,1)} %param.14) | copy-start | bytes 1572868
  26.3 7.0 %all-to-all-start.3 = ((s32[2,1,1024]{2,1,0:T(1,128)}), s32[2,1,1024]{2,1,0:T(1,128)S(1)}, u32[]{:S(2)}, u32[]{:S(2)}) async-start(s32[2,1,1024]{2,1,0:T(1,128)} %reshape.236), calls=%async_computation.3 | async-start | bytes 16384 | tf_op jit(solution)/shard_map/all_to_all | solution.py:316
  33.4 18.1 %all-to-all-start.1 = ((bf16[1,64,16,128]{3,2,0,1:T(8,128)(2,1)}), bf16[1,64,16,128]{3,2,0,1:T(8,128)(2,1)S(1)}, u32[]{:S(2)}, u32[]{:S(2)}) async-start(bf16[1,64,16,128]{3,2,0,1:T(8,128)(2,1)} %select_convert_fusion), calls=%async_computation.1 | async-start | bytes 524288 | tf_op jit(solution)/shard_map/all_to_all | solution.py:409
  56.6 15.8 %all-to-all-start.4 = ((bf16[1,64,16,128]{3,2,0,1:T(8,128)(2,1)}), bf16[1,64,16,128]{3,2,0,1:T(8,128)(2,1)S(1)}, u32[]{:S(2)}, u32[]{:S(2)}) async-start(bf16[1,64,16,128]{3,2,0,1:T(8,128)(2,1)} %get-tuple-element.17), calls=%async_computation.4 | async-start | bytes 524288 | tf_op jit(solution)/shard_map/all_to_all | solution.py:415
  89.9 3.2 %copy-start.10 = (s32[1024]{0:T(1024)S(1)}, s32[1024]{0:T(1024)}, u32[]{:S(2)}) copy-start(s32[1024]{0:T(1024)} %param.18) | copy-start | bytes 12292
  89.9 3.1 %copy-start.11 = (s32[1024]{0:T(1024)S(1)}, s32[1024]{0:T(1024)}, u32[]{:S(2)}) copy-start(s32[1024]{0:T(1024)} %param.17) | copy-start | bytes 12292
  93.0 3.2 %copy-start.16 = (f32[512,1024]{1,0:T(8,128)S(1)}, f32[512,1024]{1,0:T(8,128)}, u32[]{:S(2)}) copy-start(f32[512,1024]{1,0:T(8,128)} %fusion.56) | copy-start | bytes 6291460
  96.2 10.8 %copy-start.18 = (f32[512,512]{1,0:T(8,128)}, f32[512,512]{1,0:T(8,128)S(1)}, u32[]{:S(2)}) copy-start(f32[512,512]{1,0:T(8,128)S(1)} %fusion.22) | copy-start | bytes 3145732
  96.2 2.7 %copy-start.2 = (bf16[1024,512]{1,0:T(8,128)(2,1)S(1)}, bf16[1024,512]{1,0:T(8,128)(2,1)}, u32[]{:S(2)}) copy-start(bf16[1024,512]{1,0:T(8,128)(2,1)} %param.21) | copy-start | bytes 3145732
  98.9 1.6 copy-start.12
  98.9 1.1 copy-start.5
  103.8 0.8 copy-start.14
  107.0 1.0 copy-start.19
  107.9 1.8 copy-start.9
  114.9 3.4 %copy-start.13 = (bf16[512,1024]{1,0:T(8,128)(2,1)S(1)}, bf16[512,1024]{1,0:T(8,128)(2,1)}, u32[]{:S(2)}) copy-start(bf16[512,1024]{1,0:T(8,128)(2,1)} %copy-done.12) | copy-start | bytes 3145732
  114.9 3.4 %copy-start.15 = (bf16[512,512]{1,0:T(8,128)(2,1)S(1)}, bf16[512,512]{1,0:T(8,128)(2,1)}, u32[]{:S(2)}) copy-start(bf16[512,512]{1,0:T(8,128)(2,1)} %copy-done.14) | copy-start | bytes 1572868
  215.4 1.5 copy-start.3
  215.5 1.9 copy-start.4
  217.3 1.4 collective-permute-start.4

commit v2 on v0

v2 whole, which is shorter than its diff:
```python
import jax
import jax.numpy as jnp
from jax import lax
from jax.experimental import pallas as pl
from jax.experimental.pallas import tpu as pltpu
from jax.sharding import PartitionSpec as P

MESH = pl.DeviceIdType.MESH
bf16, f32, i32 = jnp.bfloat16, jnp.float32, jnp.int32
learn_rate = 0.5
modulus = 1000003
RING = 4
PLANE = RING * RING
CHUNKS = RING * PLANE
HALF = PLANE // 2
TOKENS = 512
HIDDEN = 1024
MINE = 512
WIDTH = 128
OWNED = 4096
SPAN = 16
ASKED = CHUNKS * SPAN
ROWBLOCK = 512

THREE, FOUR, TWO, ONE = range(4)
LANES = (512, 128, 512, 512)
ROWS = (16, 8, 16, 16)
TYPES = (bf16, f32, bf16, bf16)
STREAMS = (
    (THREE, 0, 2, 0),
    (THREE, 2, 1, 1),
    (THREE, 3, 1, 2),
    (FOUR, 0, 1, 1),
    (TWO, 0, 2, 1),
    (TWO, 2, 1, 2),
    (TWO, 3, 1, 0),
    (ONE, 0, 2, 2),
    (ONE, 2, 1, 0),
    (ONE, 3, 1, 1),
)
SLOTS = 15


class Place:
    def __init__(self, axis):
        me = lax.axis_index("dp")
        self.core = lax.axis_index("mp")
        strides = (1, RING, RING * RING)
        self.stride = strides[axis]
        self.others = (strides[(axis + 1) % 3], strides[(axis + 2) % 3])
        self.k = lax.rem(me // self.stride, RING)
        self.first = lax.rem(me // self.others[0], RING)
        self.second = lax.rem(me // self.others[1], RING)
        self.p = self.first * RING + self.second
        self.after = lax.rem(self.k + 1, RING)
        self.before = lax.rem(self.k + RING - 1, RING)
        self.opposite = lax.rem(self.k + 2, RING)
        self.right = me + (self.after - self.k) * self.stride
        self.left = me + (self.before - self.k) * self.stride

    def peer(self, p):
        return (
            self.k * self.stride
            + (p // RING) * self.others[0]
            + lax.rem(p, RING) * self.others[1]
        )


class Stream:
    def __init__(self, index, refs, places):
        self.grad, b0, nb, axis = STREAMS[index]
        self.place = places[axis]
        self.index = index
        self.lanes = pl.ds(b0 * WIDTH, nb * WIDTH)
        self.lane0, self.nlanes = b0 * WIDTH, nb * WIDTH
        g = self.grad
        for name in ("own", "other", "arrive", "total", "out", "near", "side", "part", "fan", "final"):
            setattr(self, name, refs[name][g])
        self.result = refs["result"][g]
        self.send, self.recv = refs["send"], refs["recv"]
        self.leave = refs["leave"]
        self.dtype = TYPES[g]
        self.pending = []

    def view(self, ref, first, count):
        return ref.at[pl.ds(first, count), :, self.lanes]

    def outview(self, ref, first, count):
        if self.grad != TWO:
            return self.view(ref, first, count)
        half = CHUNKS // 2
        lane = pl.multiple_of((first // half) * 512 + self.lane0, WIDTH)
        return ref.at[pl.ds(lax.rem(first, half), count), :, pl.ds(lane, self.nlanes)]

    def load(self, ref, first, count):
        return ref[pl.ds(first, count), :, self.lanes].astype(f32)

    def store(self, ref, first, count, value):
        ref[pl.ds(first, count), :, self.lanes] = value.astype(self.dtype)

    def copy(self, src, dst, slot, device):
        return pltpu.make_async_remote_copy(
            src_ref=src, dst_ref=dst,
            send_sem=self.send.at[self.index, slot], recv_sem=self.recv.at[self.index, slot],
            device_id=device, device_id_type=MESH,
        )

    def start(self, src, dst, slot, dp=None, mp=None):
        where = (
            lax.axis_index("dp") if dp is None else dp,
            self.place.core if mp is None else mp,
        )
        c = self.copy(src, dst, slot, where)
        c.start()
        self.pending.append(c)
        return c

    def swap(self):
        self.c_swap = self.start(
            self.view(self.other, 0, CHUNKS), self.view(self.arrive, 0, CHUNKS), 0,
            mp=1 - self.place.core,
        )

    def combine(self):
        self.c_swap.wait_recv()

        @pl.loop(0, CHUNKS // 8)
        def _(i):
            self.store(
                self.total, i * 8, 8,
                self.load(self.own, i * 8, 8) + self.load(self.arrive, i * 8, 8),
            )

        q = self.place
        base = q.opposite * PLANE
        self.c_na = self.start(
            self.view(self.total, base, HALF), self.view(self.near, 0, HALF), 1, dp=q.right
        )
        self.c_nb = self.start(
            self.view(self.total, base + HALF, HALF), self.view(self.near, HALF, HALF), 2, dp=q.left
        )
        self.c_sa = self.start(
            self.view(self.total, q.after * PLANE + HALF, HALF),
            self.view(self.side, HALF, HALF), 3, dp=q.right,
        )
        self.c_sb = self.start(
            self.view(self.total, q.before * PLANE, HALF),
            self.view(self.side, PLANE, HALF), 4, dp=q.left,
        )

    def relay(self):
        q = self.place
        low, high = q.after * PLANE, q.before * PLANE + HALF
        self.c_na.wait_recv()
        self.store(
            self.total, low, HALF, self.load(self.total, low, HALF) + self.load(self.near, 0, HALF)
        )
        self.c_ra = self.start(
            self.view(self.total, low, HALF), self.view(self.side, 0, HALF), 5, dp=q.right
        )
        self.c_nb.wait_recv()
        self.store(
            self.total, high, HALF,
            self.load(self.total, high, HALF) + self.load(self.near, HALF, HALF),
        )
        self.c_rb = self.start(
            self.view(self.total, high, HALF), self.view(self.side, PLANE + HALF, HALF), 6, dp=q.left
        )

    def spread(self):
        q = self.place
        for c in (self.c_sa, self.c_sb, self.c_ra, self.c_rb):
            c.wait_recv()

        @pl.loop(0, PLANE // 4)
        def _(i):
            self.store(
                self.part, i * 4, 4,
                self.load(self.total, q.k * PLANE + i * 4, 4)
                + self.load(self.side, i * 4, 4)
                + self.load(self.side, PLANE + i * 4, 4),
            )

        @pl.loop(1, PLANE)
        def _(j):
            p = lax.rem(q.p + j, PLANE)
            self.copy(
                self.view(self.part, p, 1), self.view(self.fan, j - 1, 1), 7, (q.peer(p), q.core)
            ).start()

    def wait_fan(self, slot, recv):
        fifteen = self.view(self.fan, 0, PLANE - 1)
        sem = (self.recv if recv else self.send).at[self.index, slot]
        pltpu.make_async_copy(fifteen, fifteen, sem).wait()

    def finish(self):
        q = self.place
        self.wait_fan(7, True)
        acc = self.load(self.part, q.p, 1)
        for i in range(PLANE - 1):
            acc = acc + self.load(self.fan, i, 1)
        self.store(self.final, 0, 1, acc)
        here = q.k * PLANE + q.p
        self.outview(self.out, here, 1)[...] = acc.astype(self.dtype)

        @pl.loop(1, PLANE)
        def _(j):
            p = lax.rem(q.p + j, PLANE)
            self.copy(
                self.view(self.final, 0, 1), self.outview(self.out, here, 1), 8, (q.peer(p), q.core)
            ).start()

    def share(self):
        q = self.place
        self.wait_fan(8, True)
        low = self.outview(self.out, q.k * PLANE, HALF)
        high = self.outview(self.out, q.k * PLANE + HALF, HALF)
        self.c_gl = self.start(low, low, 9, dp=q.right)
        self.c_gh = self.start(high, high, 10, dp=q.left)
        self.c_hh = self.start(high, high, 11, dp=q.right)
        self.c_hl = self.start(low, low, 12, dp=q.left)

    def forward(self):
        q = self.place
        self.c_gl.wait_recv()
        low = self.outview(self.out, q.before * PLANE, HALF)
        self.c_fl = self.start(low, low, 13, dp=q.right)
        self.c_gh.wait_recv()
        high = self.outview(self.out, q.after * PLANE + HALF, HALF)
        self.c_fh = self.start(high, high, 14, dp=q.left)

    def close(self):
        for c in (self.c_hh, self.c_hl, self.c_fl, self.c_fh):
            c.wait_recv()
        if self.grad == TWO:
            ends = [(0, self.lane0), (0, 512 + self.lane0)]
            count = CHUNKS // 2
        else:
            ends, count = [(0, self.lane0)], CHUNKS
        self.leaving = []
        for n, (first, lane) in enumerate(ends):
            where = (pl.ds(first, count), slice(None), pl.ds(lane, self.nlanes))
            c = pltpu.make_async_copy(
                self.out.at[where], self.result.at[where], self.leave.at[self.index, n]
            )
            c.start()
            self.leaving.append(c)

    def drain(self):
        for c in self.pending:
            c.wait_send()
        self.wait_fan(7, False)
        self.wait_fan(8, False)
        for c in self.leaving:
            c.wait()


class Group:
    def __init__(self, streams):
        self.streams = streams

    def __getattr__(self, step):
        def run():
            for s in self.streams:
                getattr(s, step)()
        return run


def rows_by_columns(a, b):
    return lax.dot_general(a, b, (((0,), (0,)), ((), ())), preferred_element_type=f32)


def times_transposed(a, b):
    return lax.dot_general(a, b, (((1,), (1,)), ((), ())), preferred_element_type=f32)


def tile(n, size=256):
    return pl.ds(pl.multiple_of(n * size, size), size)


def step_kernel(
    asked, ids, mult, add, w1, w2, w3, w4, ccot, hcot, table,
    r3, r4, r2, r1, hot_out, table_out, emb_out,
    *rest,
):
    names = ("own", "other", "arrive", "total", "near", "side", "part", "fan", "final", "out")
    refs = {name: rest[4 * i : 4 * i + 4] for i, name in enumerate(names)}
    rest = rest[4 * len(names) :]
    (
        refs["send"], refs["recv"], refs["leave"],
        w1c, w2c, w3c, w4c, feats, a1, a2, a3, ds1, ds2, ds3, b1, b2, b3, cot, emb,
        tab, tabt, newtab, rowmsg, rowbuf, rowsum, hc, carr, onehot, embt, ebuf, hout,
        loads, wsend, wrecv, hsend, hrecv, stores,
    ) = rest
    refs["result"] = (r3, r4, r2, r1)
    me = lax.axis_index("dp")
    core = lax.axis_index("mp")
    partner = (me, 1 - core)
    places = [Place(a) for a in range(3)]
    streams = [Stream(i, refs, places) for i in range(len(STREAMS))]
    first, second, third = Group(streams[:4]), Group(streams[4:7]), Group(streams[7:])

    load = {}
    for n, (name, src, dst) in enumerate((
        ("w1", w1, w1c.at[:, pl.ds(0, MINE)]),
        ("w2", w2, w2c.at[pl.ds(0, MINE)]),
        ("w3", w3, w3c.at[:, pl.ds(0, MINE)]),
        ("w4", w4, w4c.at[pl.ds(0, MINE)]),
        ("hcot", hcot.at[0, :, pl.ds(pl.multiple_of(core * SPAN, SPAN), SPAN)], hc),
        ("cot", ccot.at[pl.ds(pl.multiple_of(core * TOKENS, TOKENS), TOKENS)], cot),
        ("table", table, tab),
    )):
        load[name] = pltpu.make_async_copy(src, dst, loads.at[n])
        load[name].start()

    barrier = pltpu.get_barrier_semaphore()
    pl.semaphore_signal(barrier, inc=1, device_id=partner, device_id_type=MESH)

    @pl.loop(1, CHUNKS)
    def _(j):
        pl.semaphore_signal(
            barrier, inc=1, device_id=(lax.rem(me + j, CHUNKS), core), device_id_type=MESH
        )

    lane = lax.broadcasted_iota(i32, (CHUNKS, WIDTH), 1)
    begin = core * SPAN
    want = jnp.where((lane >= begin) & (lane < begin + SPAN), asked[...], 0)
    shift = lax.rem(lax.rem(me, 8) * SPAN - begin + WIDTH, WIDTH)
    want = pltpu.roll(want, shift, 1)
    rowmsg[...] = jnp.broadcast_to(want[:, None, :], (CHUNKS, 8, WIDTH))

    for b in range(TOKENS // WIDTH):
        line = ids[pl.ds(core * (TOKENS // WIDTH) + b, 1), :]
        column = jnp.transpose(jnp.broadcast_to(line, (WIDTH, WIDTH)))

        @pl.loop(0, HIDDEN // WIDTH)
        def _(j, b=b, column=column):
            h = column * mult[pl.ds(j, 1), :] + add[pl.ds(j, 1), :]
            q = (h.astype(f32) * (1.0 / modulus)).astype(i32)
            r = h - q * modulus
            r = jnp.where(r < 0, r + modulus, r)
            r = jnp.where(r >= modulus, r - modulus, r)
            feats[pl.ds(b * WIDTH, WIDTH), tile(j, WIDTH)] = (
                r.astype(f32) * (2.0 / 1000002.0) - 1.0
            ).astype(bf16)

    pl.semaphore_wait(barrier, CHUNKS)

    sent = []

    def give(src, dst, n, device):
        c = pltpu.make_async_remote_copy(
            src_ref=src, dst_ref=dst, send_sem=wsend.at[n], recv_sem=wrecv.at[n],
            device_id=device, device_id_type=MESH,
        )
        c.start()
        sent.append(c)
        return c

    mine, theirs = pl.ds(0, MINE), pl.ds(MINE, MINE)
    load["w1"].wait()
    got1 = give(w1c.at[:, mine], w1c.at[:, theirs], 0, partner)
    load["w2"].wait()
    got2 = give(w2c.at[mine], w2c.at[theirs], 1, partner)
    load["w3"].wait()
    got3 = give(w3c.at[:, mine], w3c.at[:, theirs], 2, partner)
    load["w4"].wait()
    got4 = give(w4c.at[mine], w4c.at[theirs], 3, partner)

    load["hcot"].wait()

    def hot(src, dst, n, s):
        return pltpu.make_async_remote_copy(
            src_ref=src, dst_ref=dst, send_sem=hsend.at[n], recv_sem=hrecv.at[n],
            device_id=(s, core), device_id_type=MESH,
        )

    @pl.loop(1, CHUNKS)
    def _(j):
        o = lax.rem(me + j, CHUNKS)
        hot(rowmsg.at[o], rowbuf.at[me], 0, o).start()
        hot(hc.at[o], carr.at[0, me], 1, o).start()

    rowbuf[pl.ds(me, 1)] = rowmsg[pl.ds(me, 1)]
    carr[0, pl.ds(me, 1)] = hc[pl.ds(me, 1)]

    def hot_wait(ref, n, recv):
        sem = (hrecv if recv else hsend).at[n]
        part = ref.at[pl.ds(0, CHUNKS - 1)]
        pltpu.make_async_copy(part, part, sem).wait()

    def activate(pre, act, ds, columns):
        sig = 0.5 * jnp.tanh(0.5 * pre) + 0.5
        act[:, columns] = (pre * sig).astype(bf16)
        ds[:, columns] = sig * (1.0 + pre * (1.0 - sig))

    def layer(src, w, act, ds, lo, hi):
        @pl.loop(lo, hi)
        def _(n):
            pre = jnp.dot(src[...], w[:, tile(n)], preferred_element_type=f32)
            activate(pre, act, ds, tile(n))

    layer(feats, w1c, a1, ds1, 0, 2)
    got1.wait_recv()
    layer(feats, w1c, a1, ds1, 2, 4)
    got2.wait_recv()
    layer(a1, w2c, a2, ds2, 0, 4)
    layer(a2, w3c, a3, ds3, 0, 2)
    got3.wait_recv()
    layer(a2, w3c, a3, ds3, 2, 4)
    got4.wait_recv()
    load["cot"].wait()

    @pl.loop(0, 4)
    def _(n):
        b3[:, tile(n)] = (times_transposed(cot[...], w4c[tile(n), :]) * ds3[:, tile(n)]).astype(bf16)

    def tall_grad(act, back, g, half, ref):
        @pl.loop(0, 4)
        def _(m):
            t = rows_by_columns(act[:, tile(m)], back[:, pl.ds(half * MINE, MINE)])
            ref[g][pl.ds(m * 16, 16)] = t.reshape(16, 16, 512).astype(ref[g].dtype)

    def wide_grad(half, ref):
        @pl.loop(0, 2)
        def _(m):
            for h in range(2):
                t = rows_by_columns(a1[:, tile(m + 2 * half)], b2[:, pl.ds(h * 512, 512)])
                ref[TWO][pl.ds(h * 32 + m * 16, 16)] = t.reshape(16, 16, 512).astype(ref[TWO].dtype)

    def grad_four(half, ref):
        t = rows_by_columns(a3[:, pl.ds(half * MINE, MINE)], cot[...])
        ref[FOUR][...] = t.reshape(CHUNKS, 8, WIDTH)

    own, other = refs["own"], refs["other"]
    tall_grad(a2, b3, THREE, 1, other)
    grad_four(1, other)
    first.swap()
    tall_grad(a2, b3, THREE, 0, own)
    grad_four(0, own)
    first.combine()

    @pl.loop(0, 4)
    def _(n):
        b2[:, tile(n)] = (times_transposed(b3[...], w3c[tile(n), :]) * ds2[:, tile(n)]).astype(bf16)

    wide_grad(1, other)
    second.swap()
    first.relay()
    wide_grad(0, own)
    second.combine()

    @pl.loop(0, 4)
    def _(n):
        b1[:, tile(n)] = (times_transposed(b2[...], w2c[tile(n), :]) * ds1[:, tile(n)]).astype(bf16)

    tall_grad(feats, b1, ONE, 1, other)
    third.swap()
    first.spread()
    second.relay()
    tall_grad(feats, b1, ONE, 0, own)
    third.combine()

    emb[core] = jnp.dot(a3[...], w4c[...], preferred_element_type=f32).astype(bf16)
    got_emb = give(emb.at[core], emb.at[core], 4, partner)

    hot_wait(rowbuf, 0, True)
    for g in range(8):
        total = rowbuf[8 * g]
        for i in range(1, 8):
            total = total + rowbuf[8 * g + i]
        rowsum[0, g] = total
    got_rows = give(rowsum.at[0], rowsum.at[1], 5, partner)
    hot_wait(carr.at[0], 1, True)
    got_carr = give(carr.at[0], carr.at[1], 6, partner)
    first.finish()
    load["table"].wait()

    @pl.loop(0, OWNED // WIDTH)
    def _(n):
        tabt[:, tile(n, WIDTH)] = jnp.transpose(tab[tile(n, WIDTH), :]).astype(bf16)

    def select(which, block):
        row = lax.broadcasted_iota(i32, (ROWBLOCK, WIDTH), 0) + (block * ROWBLOCK + 1)
        for g in range(8):
            hit = row == jnp.broadcast_to(rowsum[which, g][0:1, :], (ROWBLOCK, WIDTH))
            onehot[:, pl.ds(g * WIDTH, WIDTH)] = jnp.where(hit, 1.0, 0.0).astype(bf16)

    second.spread()
    third.relay()
    embt[...] = jnp.zeros_like(embt)

    @pl.loop(0, OWNED // ROWBLOCK)
    def _(n):
        select(0, n)
        embt[...] += jnp.dot(tabt[:, tile(n, ROWBLOCK)], onehot[...], preferred_element_type=f32)

    for g in range(8):
        found = jnp.transpose(embt[:, pl.ds(g * WIDTH, WIDTH)]).astype(bf16)
        ebuf[pl.ds(g * 8, 8)] = found.reshape(8, SPAN, WIDTH)

    @pl.loop(1, CHUNKS)
    def _(j):
        s = lax.rem(me + j, CHUNKS)
        hot(ebuf.at[s], hout.at[me, core], 2, s).start()

    hout[pl.ds(me, 1), pl.ds(core, 1)] = ebuf[pl.ds(me, 1)][:, None]

    first.share()
    second.finish()
    third.spread()
    got_rows.wait_recv()
    got_carr.wait_recv()

    def update(lo, hi):
        @pl.loop(lo, hi)
        def _(n):
            rows = tile(n, ROWBLOCK)
            select(0, n)
            delta = jnp.dot(onehot[...], carr[0].reshape(ASKED, WIDTH), preferred_element_type=f32)
            select(1, n)
            delta += jnp.dot(onehot[...], carr[1].reshape(ASKED, WIDTH), preferred_element_type=f32)
            newtab[rows, :] = tab[rows, :] - learn_rate * delta

    update(0, 2)
    first.forward()
    second.share()
    third.finish()
    update(2, 4)
    first.close()
    second.forward()
    third.share()
    update(4, 6)
    third.forward()
    hot_wait(hout.at[:, 0], 2, True)
    got_hot = give(hout.at[:, core], hout.at[:, core], 7, partner)
    update(6, 8)
    put_table = pltpu.make_async_copy(newtab, table_out, stores.at[0])
    put_table.start()
    second.close()
    got_emb.wait_recv()
    put_emb = pltpu.make_async_copy(emb, emb_out, stores.at[1])
    put_emb.start()
    got_hot.wait_recv()
    put_hot = pltpu.make_async_copy(hout, hot_out, stores.at[2])
    put_hot.start()
    third.close()

    for group in (first, second, third):
        group.drain()
    for c in sent:
        c.wait_send()
    hot_wait(rowbuf, 0, False)
    hot_wait(carr.at[0], 1, False)
    hot_wait(ebuf, 2, False)
    for c in (put_table, put_emb, put_hot):
        c.wait()


def shapes(count, types=TYPES):
    return [pltpu.VMEM((count, ROWS[g], LANES[g]), types[g]) for g in range(4)]


def outs(kind):
    sizes = [(CHUNKS, ROWS[g], LANES[g]) for g in range(4)]
    sizes[TWO] = (CHUNKS // 2, 16, 1024)
    return [kind(sizes[g], TYPES[g]) for g in range(4)]


def step(*args):
    vmem = pl.BlockSpec(memory_space=pltpu.VMEM)
    anywhere = pl.BlockSpec(memory_space=pl.ANY)
    dma = pltpu.SemaphoreType.DMA
    square = (HIDDEN, HIDDEN)
    tokens = (TOKENS, HIDDEN)
    return pl.pallas_call(
        step_kernel,
        out_shape=outs(jax.ShapeDtypeStruct) + [
            jax.ShapeDtypeStruct((CHUNKS, 2, SPAN, WIDTH), bf16),
            jax.ShapeDtypeStruct((OWNED, WIDTH), f32),
            jax.ShapeDtypeStruct((2, TOKENS, WIDTH), bf16),
        ],
        in_specs=[vmem] * 4 + [anywhere] * 7,
        out_specs=[anywhere] * 7,
        scratch_shapes=(
            shapes(CHUNKS, (f32,) * 4)
            + shapes(CHUNKS)
            + shapes(CHUNKS)
            + shapes(CHUNKS)
            + shapes(PLANE)
            + shapes(2 * PLANE)
            + shapes(PLANE)
            + shapes(PLANE - 1)
            + shapes(1)
            + outs(pltpu.VMEM)
            + [dma((len(STREAMS), SLOTS)), dma((len(STREAMS), SLOTS)), dma((len(STREAMS), 2))]
            + [pltpu.VMEM(square, bf16)] * 3
            + [pltpu.VMEM((HIDDEN, WIDTH), bf16)]
            + [pltpu.VMEM(tokens, bf16)] * 4
            + [pltpu.VMEM(tokens, f32)] * 3
            + [pltpu.VMEM(tokens, bf16)] * 3
            + [
                pltpu.VMEM((TOKENS, WIDTH), bf16),
                pltpu.VMEM((2, TOKENS, WIDTH), bf16),
                pltpu.VMEM((OWNED, WIDTH), f32),
                pltpu.VMEM((WIDTH, OWNED), bf16),
                pltpu.VMEM((OWNED, WIDTH), f32),
                pltpu.VMEM((CHUNKS, 8, WIDTH), i32),
                pltpu.VMEM((CHUNKS, 8, WIDTH), i32),
                pltpu.VMEM((2, 8, 8, WIDTH), i32),
                pltpu.VMEM((CHUNKS, SPAN, WIDTH), bf16),
                pltpu.VMEM((2, CHUNKS, SPAN, WIDTH), bf16),
                pltpu.VMEM((ROWBLOCK, ASKED), bf16),
                pltpu.VMEM((WIDTH, ASKED), f32),
                pltpu.VMEM((CHUNKS, SPAN, WIDTH), bf16),
                pltpu.VMEM((CHUNKS, 2, SPAN, WIDTH), bf16),
                dma((7,)), dma((8,)), dma((8,)), dma((3,)), dma((3,)), dma((3,)),
            ]
        ),
        compiler_params=pltpu.CompilerParams(
            collective_id=0, has_side_effects=True, vmem_limit_bytes=67043328
        ),
        name="step",
    )(*args)


def local(
    hot_rows, hot_count, hot_cot, table, cold_ids, hash_mult, hash_add,
    layer_one, layer_two, layer_three, layer_four, cold_cot,
):
    slots = jnp.arange(hot_rows.shape[2], dtype=i32)
    asked = jnp.where(slots[None, :] < hot_count[0][:, None], hot_rows[0] + 1, 0)
    asked = jnp.pad(asked, ((0, 0), (0, WIDTH - asked.shape[1])))
    r3, r4, r2, r1, hot_emb, new_table, cold_emb = step(
        asked, cold_ids.reshape(8, WIDTH), hash_mult.reshape(8, WIDTH), hash_add.reshape(8, WIDTH),
        layer_one, layer_two, layer_three, layer_four, cold_cot, hot_cot, table,
    )
    factor = float(cold_ids.shape[0] * lax.axis_size("dp")) ** (-0.5)
    return (
        hot_emb.reshape(hot_cot.shape),
        new_table,
        cold_emb.reshape(cold_cot.shape),
        r1.reshape(layer_one.shape).astype(f32) * factor,
        r2.reshape(layer_two.shape).astype(f32) * factor,
        r3.reshape(layer_three.shape).astype(f32) * factor,
        r4.reshape(layer_four.shape) * factor,
    )


def solution(mesh):
    in_specs = (
        P("dp", None, None),
        P("dp", None),
        P("dp", None, None, None),
        P("dp", None),
        P("dp"),
        P(),
        P(),
        P(None, "mp"),
        P("mp", None),
        P(None, "mp"),
        P("mp", None),
        P("dp", None),
    )
    out_specs = (
        P("dp", None, None, None),
        P("dp", None),
        P("dp", None),
        P(None, "mp"),
        P("mp", None),
        P(None, "mp"),
        P("mp", None),
    )
    return jax.shard_map(local, mesh=mesh, in_specs=in_specs, out_specs=out_specs, check_vma=False)
```

time: 271 us -> 91.6 us (0.34)
  waiting for transfers between devices: 129 us -> 0 us
  Pallas kernels: 0 us -> 79.1 us
  other arithmetic: 43.4 us -> 7.33 us
  matrix products: 30.2 us -> 0 us
  starting transfers between devices: 24 us -> 0 us
  between operations: 14.1 us -> 0.67 us
  blocking collectives: 12.9 us -> 0 us
  local copies, waits for them, and re-layouts: 16.5 us -> 4.26 us
    pallas_call x0 -> x1, Pallas kernels: none -> 79.1 us  [step(): pl.pallas_call(step_kernel, out_shape=outs(jax.ShapeDtypeStruct) + [jax.S...]
    psum x1 -> x0, waiting for transfers between devices: 55.6 us -> none  [local(): lax.psum((part_one, part_two, part_three, part_four), 'dp')]
    all_gather x2 -> x0, waiting for transfers between devices: 43.6 us -> none  [over_pieces(): return lax.all_gather(array, axis).sum(0)]
    dot_general x10 -> x0, matrix products: 30.2 us -> none  [the longest x1 8.12 us: local(): jnp.dot(feats.T, back_one, preferred_element_type=jnp.float32) * factor]
    all_to_all x4 -> x0, waiting for transfers between devices: 29.3 us -> none  [the longest x1 10.1 us: local(): lax.all_to_all(own_cot, 'dp', split_axis=1, concat_axis=1, tiled=True)]
    all_to_all x4 -> x0, starting transfers between devices: 23.7 us -> none  [the longest x1 10.4 us: local(): lax.all_to_all(mine, 'dp', split_axis=1, concat_axis=1, tiled=True)]
    reduce_sum x3 -> x0, other arithmetic: 14.1 us -> none  [the longest x2 13.3 us: over_pieces(): return lax.all_gather(array, axis).sum(0)]
    scatter-add x1 -> x0, other arithmetic: 13.2 us -> none  [local(): delta = jnp.zeros_like(table).at[received.reshape(-1)].add(arrived.reshap...]
  transfers between devices with their start and end apart: 7 -> 0, of which waited for: 6 -> 0; matrix products, arithmetic and copies ran while one was open for 13% -> 0% of each run, Pallas kernels for 0% -> 0%
where the time goes in v2:
time: 91.6 us; the launch traced here: 91.4 us
  Pallas kernels  79.1 us (86%)
  other arithmetic  7.33 us (8%)
  local copies, waits for them, and re-layouts  4.26 us (5%)
    pallas_call x1, Pallas kernels, step(): pl.pallas_call(step_kernel, out_shape=outs(jax.ShapeDtypeStruct) + [jax.S...  79.1 us
    mul x1, other arithmetic, local(): r3.reshape(layer_three.shape).astype(f32) * factor  4.28 us
    unnamed x14, local copies, waits for them, and re-layouts  3.63 us

profile of v2, /device:TPU:0, one launch (start us, length us, event | category | flops | bytes accessed | tf_op | source)
XLA Modules:
  0.0 91.4 jit_solution(6186583836274750254)
XLA Ops:
  0.6 0.8 copy.19
  1.4 0.7 bitcast_select_fusion
  2.2 0.6 pad.4.asked
  2.8 79.1 %step.1 = (bf16[64,16,512]{2,1,0:T(8,128)(2,1)}, f32[64,8,128]{2,1,0:T(8,128)}, bf16[32,16,1024]{2,1,0:T(8,128)(2,1)}, bf16[64,16,512]{2,1,0:T(8,128)(2,1)}, bf1...) custom-call(s32[64,128]{1,0:T(8,128)} %pad.4.asked, s32[8,128]{1,0:T(8,128)} %bitcast.18, ...), custom_call_target="tpu_custom_call" | custom-call | tf_op jit(solution)/shard_map/step/pallas_call | solution.py:576
  81.9 0.0 copy-start.1
  81.9 4.3 %convert_multiply_fusion = (f32[64,16,512]{2,1,0:T(8,128)}, f32[64,16,512]{2,1,0:T(8,128)}) fusion(bf16[64,16,512]{2,1,0:T(8,128)(2,1)} %get-tuple-element.19, bf16[64,16,512]{2,1,0:T(8,128)(2,1)} %get-tuple-element.17), kind=kLoop, calls=%fused_computation | loop fusion | flops 2097152 | bytes 6291456 | tf_op jit(solution)/shard_map/mul | solution.py:645
  86.2 0.0 copy-start.4
  86.2 0.0 copy-start.2
  86.2 0.0 copy-done.1
  86.2 0.0 copy-start
  86.2 1.6 %convert_multiply_fusion.1 = f32[32,16,1024]{2,1,0:T(8,128)} fusion(bf16[32,16,1024]{2,1,0:T(8,128)(2,1)S(1)} %copy-done.1), kind=kLoop, calls=%fused_computation.1 | loop fusion | flops 1048576 | bytes 3145728 | tf_op jit(solution)/shard_map/mul | solution.py:644
  87.8 0.0 copy-done.4
  87.8 0.7 multiply_bitcast_fusion
  88.5 0.0 copy-done.2
  88.6 0.8 copy.23
  89.3 0.0 copy-done
  89.3 0.0 copy-start.3
  89.4 1.3 %copy.24 = f32[4096,128]{1,0:T(8,128)} copy(f32[4096,128]{1,0:T(8,128)S(1)} %copy-done) | data formatting | bytes 4194304
  90.7 0.0 copy-done.3
  90.7 0.7 copy.25
Async XLA Ops:
  81.9 4.3 %copy-start.1 = (bf16[32,16,1024]{2,1,0:T(8,128)(2,1)S(1)}, bf16[32,16,1024]{2,1,0:T(8,128)(2,1)}, u32[]{:S(2)}) copy-start(bf16[32,16,1024]{2,1,0:T(8,128)(2,1)} %get-tuple-element.18) | copy-start | bytes 3145732
  86.2 1.6 %copy-start.4 = (f32[64,8,128]{2,1,0:T(8,128)S(1)}, f32[64,8,128]{2,1,0:T(8,128)}, u32[]{:S(2)}) copy-start(f32[64,8,128]{2,1,0:T(8,128)} %get-tuple-element.20) | copy-start | bytes 786436
  86.2 2.3 %copy-start.2 = (bf16[64,2,16,128]{3,2,1,0:T(8,128)(2,1)S(1)}, bf16[64,2,16,128]{3,2,1,0:T(8,128)(2,1)}, u32[]{:S(2)}) copy-start(bf16[64,2,16,128]{3,2,1,0:T(8,128)(2,1)} %get-tuple-element.14) | copy-start | bytes 1572868
  86.2 3.1 %copy-start = (f32[4096,128]{1,0:T(8,128)S(1)}, f32[4096,128]{1,0:T(8,128)}, u32[]{:S(2)}) copy-start(f32[4096,128]{1,0:T(8,128)} %get-tuple-element.31) | copy-start | bytes 6291460
  89.3 1.3 %copy-start.3 = (bf16[2,512,128]{2,1,0:T(8,128)(2,1)S(1)}, bf16[2,512,128]{2,1,0:T(8,128)(2,1)}, u32[]{:S(2)}) copy-start(bf16[2,512,128]{2,1,0:T(8,128)(2,1)} %get-tuple-element.16) | copy-start | bytes 786436

commit v3 on v2

--- a/solution.py
+++ b/solution.py
@@ -48,9 +48,9 @@
         strides = (1, RING, RING * RING)
         self.stride = strides[axis]
         self.others = (strides[(axis + 1) % 3], strides[(axis + 2) % 3])
-        self.k = lax.rem(me // self.stride, RING)
-        self.first = lax.rem(me // self.others[0], RING)
-        self.second = lax.rem(me // self.others[1], RING)
+        self.k = lax.rem(lax.div(me, self.stride), RING)
+        self.first = lax.rem(lax.div(me, self.others[0]), RING)
+        self.second = lax.rem(lax.div(me, self.others[1]), RING)
         self.p = self.first * RING + self.second
         self.after = lax.rem(self.k + 1, RING)
         self.before = lax.rem(self.k + RING - 1, RING)
@@ -61,7 +61,7 @@
     def peer(self, p):
         return (
             self.k * self.stride
-            + (p // RING) * self.others[0]
+            + lax.div(p, RING) * self.others[0]
             + lax.rem(p, RING) * self.others[1]
         )
 
@@ -76,9 +76,7 @@
         g = self.grad
         for name in ("own", "other", "arrive", "total", "out", "near", "side", "part", "fan", "final"):
             setattr(self, name, refs[name][g])
-        self.result = refs["result"][g]
         self.send, self.recv = refs["send"], refs["recv"]
-        self.leave = refs["leave"]
         self.dtype = TYPES[g]
         self.pending = []
 
@@ -89,7 +87,7 @@
         if self.grad != TWO:
             return self.view(ref, first, count)
         half = CHUNKS // 2
-        lane = pl.multiple_of((first // half) * 512 + self.lane0, WIDTH)
+        lane = pl.multiple_of(lax.div(first, half) * 512 + self.lane0, WIDTH)
         return ref.at[pl.ds(lax.rem(first, half), count), :, pl.ds(lane, self.nlanes)]
 
     def load(self, ref, first, count):
@@ -124,7 +122,7 @@
     def combine(self):
         self.c_swap.wait_recv()
 
-        @pl.loop(0, CHUNKS // 8)
+        @pl.loop(0, CHUNKS // 8, unroll=2)
         def _(i):
             self.store(
                 self.total, i * 8, 8,
@@ -172,7 +170,7 @@
         for c in (self.c_sa, self.c_sb, self.c_ra, self.c_rb):
             c.wait_recv()
 
-        @pl.loop(0, PLANE // 4)
+        @pl.loop(0, PLANE // 4, unroll=2)
         def _(i):
             self.store(
                 self.part, i * 4, 4,
@@ -181,7 +179,7 @@
                 + self.load(self.side, PLANE + i * 4, 4),
             )
 
-        @pl.loop(1, PLANE)
+        @pl.loop(1, PLANE, unroll=5)
         def _(j):
             p = lax.rem(q.p + j, PLANE)
             self.copy(
@@ -203,7 +201,7 @@
         here = q.k * PLANE + q.p
         self.outview(self.out, here, 1)[...] = acc.astype(self.dtype)
 
-        @pl.loop(1, PLANE)
+        @pl.loop(1, PLANE, unroll=5)
         def _(j):
             p = lax.rem(q.p + j, PLANE)
             self.copy(
@@ -232,27 +230,12 @@
     def close(self):
         for c in (self.c_hh, self.c_hl, self.c_fl, self.c_fh):
             c.wait_recv()
-        if self.grad == TWO:
-            ends = [(0, self.lane0), (0, 512 + self.lane0)]
-            count = CHUNKS // 2
-        else:
-            ends, count = [(0, self.lane0)], CHUNKS
-        self.leaving = []
-        for n, (first, lane) in enumerate(ends):
-            where = (pl.ds(first, count), slice(None), pl.ds(lane, self.nlanes))
-            c = pltpu.make_async_copy(
-                self.out.at[where], self.result.at[where], self.leave.at[self.index, n]
-            )
-            c.start()
-            self.leaving.append(c)
 
     def drain(self):
         for c in self.pending:
             c.wait_send()
         self.wait_fan(7, False)
         self.wait_fan(8, False)
-        for c in self.leaving:
-            c.wait()
 
 
 class Group:
@@ -279,20 +262,22 @@
 
 
 def step_kernel(
-    asked, ids, mult, add, w1, w2, w3, w4, ccot, hcot, table,
-    r3, r4, r2, r1, hot_out, table_out, emb_out,
+    rows_in, count_in, ids_in, mult_in, add_in, w1, w2, w3, w4, ccot, hcot, table,
+    r3, r4, r2, r1, hout, newtab, emb,
     *rest,
 ):
-    names = ("own", "other", "arrive", "total", "near", "side", "part", "fan", "final", "out")
+    names = ("other", "arrive", "total", "near", "side", "part", "fan", "final")
     refs = {name: rest[4 * i : 4 * i + 4] for i, name in enumerate(names)}
     rest = rest[4 * len(names) :]
     (
-        refs["send"], refs["recv"], refs["leave"],
-        w1c, w2c, w3c, w4c, feats, a1, a2, a3, ds1, ds2, ds3, b1, b2, b3, cot, emb,
-        tab, tabt, newtab, rowmsg, rowbuf, rowsum, hc, carr, onehot, embt, ebuf, hout,
-        loads, wsend, wrecv, hsend, hrecv, stores,
+        refs["send"], refs["recv"], own_large, own_four,
+        w1c, w2c, w3c, w4c, feats, a1, a2, a3, ds1, ds2, ds3, b2, b3, cot,
+        tab, tabt, spare, rowmsg, rowbuf, rowsum, hc, carr, onehot, twohot, embt, ebuf,
+        loads, wsend, wrecv, hsend, hrecv, rows, count, ids, mult, add,
     ) = rest
-    refs["result"] = (r3, r4, r2, r1)
+    b1 = b3
+    refs["out"] = (r3, r4, r2, r1)
+    refs["own"] = (own_large, own_four, own_large, own_large)
     me = lax.axis_index("dp")
     core = lax.axis_index("mp")
     partner = (me, 1 - core)
@@ -302,6 +287,11 @@
 
     load = {}
     for n, (name, src, dst) in enumerate((
+        ("rows", rows_in, rows),
+        ("count", count_in, count),
+        ("ids", ids_in, ids),
+        ("mult", mult_in, mult),
+        ("add", add_in, add),
         ("w1", w1, w1c.at[:, pl.ds(0, MINE)]),
         ("w2", w2, w2c.at[pl.ds(0, MINE)]),
         ("w3", w3, w3c.at[:, pl.ds(0, MINE)]),
@@ -316,29 +306,32 @@
     barrier = pltpu.get_barrier_semaphore()
     pl.semaphore_signal(barrier, inc=1, device_id=partner, device_id_type=MESH)
 
-    @pl.loop(1, CHUNKS)
+    @pl.loop(1, CHUNKS, unroll=7)
     def _(j):
         pl.semaphore_signal(
             barrier, inc=1, device_id=(lax.rem(me + j, CHUNKS), core), device_id_type=MESH
         )
 
-    lane = lax.broadcasted_iota(i32, (CHUNKS, WIDTH), 1)
-    begin = core * SPAN
-    want = jnp.where((lane >= begin) & (lane < begin + SPAN), asked[...], 0)
-    shift = lax.rem(lax.rem(me, 8) * SPAN - begin + WIDTH, WIDTH)
-    want = pltpu.roll(want, shift, 1)
+    for name in ("rows", "count", "ids", "mult", "add"):
+        load[name].wait()
+    slot = lax.broadcasted_iota(i32, (SPAN, CHUNKS), 0) + core * SPAN
+    want = rows[0, pl.ds(pl.multiple_of(core * SPAN, SPAN), SPAN), :] + 1
+    spare[...] = jnp.zeros_like(spare)
+    spare[pl.ds(pl.multiple_of(lax.rem(me, 8) * SPAN, SPAN), SPAN), pl.ds(0, CHUNKS)] = jnp.where(
+        slot < count[...], want, 0
+    )
+    want = jnp.transpose(spare[...])[:CHUNKS]
     rowmsg[...] = jnp.broadcast_to(want[:, None, :], (CHUNKS, 8, WIDTH))
 
     for b in range(TOKENS // WIDTH):
         line = ids[pl.ds(core * (TOKENS // WIDTH) + b, 1), :]
         column = jnp.transpose(jnp.broadcast_to(line, (WIDTH, WIDTH)))
 
-        @pl.loop(0, HIDDEN // WIDTH)
+        @pl.loop(0, HIDDEN // WIDTH, unroll=2)
         def _(j, b=b, column=column):
             h = column * mult[pl.ds(j, 1), :] + add[pl.ds(j, 1), :]
-            q = (h.astype(f32) * (1.0 / modulus)).astype(i32)
+            q = (h.astype(f32) * ((1.0 - 4e-7) / modulus)).astype(i32)
             r = h - q * modulus
-            r = jnp.where(r < 0, r + modulus, r)
             r = jnp.where(r >= modulus, r - modulus, r)
             feats[pl.ds(b * WIDTH, WIDTH), tile(j, WIDTH)] = (
                 r.astype(f32) * (2.0 / 1000002.0) - 1.0
@@ -359,50 +352,61 @@
 
     mine, theirs = pl.ds(0, MINE), pl.ds(MINE, MINE)
     load["w1"].wait()
-    got1 = give(w1c.at[:, mine], w1c.at[:, theirs], 0, partner)
+    got1 = [
+        give(w1c.at[:, pl.ds(256 * n, 256)], w1c.at[:, pl.ds(MINE + 256 * n, 256)], n, partner)
+        for n in range(2)
+    ]
     load["w2"].wait()
-    got2 = give(w2c.at[mine], w2c.at[theirs], 1, partner)
+    got2 = give(w2c.at[mine], w2c.at[theirs], 9, partner)
+
+    load["table"].wait()
+
+    @pl.loop(0, OWNED // WIDTH, unroll=8)
+    def _(n):
+        tabt[:, tile(n, WIDTH)] = jnp.transpose(tab[tile(n, WIDTH), :]).astype(bf16)
+
+    load["hcot"].wait()
+
+    def hot(src, dst, n, s):
+        return pltpu.make_async_remote_copy(
+            src_ref=src, dst_ref=dst, send_sem=hsend.at[n], recv_sem=hrecv.at[n],
+            device_id=(s, core), device_id_type=MESH,
+        )
+
+    @pl.loop(1, CHUNKS, unroll=7)
+    def _(j):
+        o = lax.rem(me + j, CHUNKS)
+        hot(rowmsg.at[o], rowbuf.at[me], 0, o).start()
+        hot(hc.at[o], carr.at[0, me], 1, o).start()
+
+    rowbuf[pl.ds(me, 1)] = rowmsg[pl.ds(me, 1)]
+    carr[0, pl.ds(me, 1)] = hc[pl.ds(me, 1)]
+
+    def hot_wait(ref, n, recv):
+        sem = (hrecv if recv else hsend).at[n]
+        part = ref.at[pl.ds(0, CHUNKS - 1)]
+        pltpu.make_async_copy(part, part, sem).wait()
+
+    def activate(pre, act, ds, columns):
+        sig = 0.5 * jnp.tanh(0.5 * pre) + 0.5
+        act[:, columns] = (pre * sig).astype(bf16)
+        ds[:, columns] = sig * (1.0 + pre * (1.0 - sig))
+
+    def layer(src, w, act, ds, lo, hi):
+        for n in range(lo, hi):
+            columns = pl.ds(n * 256, 256)
+            pre = jnp.dot(src[...], w[:, columns], preferred_element_type=f32)
+            activate(pre, act, ds, columns)
+
+    layer(feats, w1c, a1, ds1, 0, 2)
     load["w3"].wait()
     got3 = give(w3c.at[:, mine], w3c.at[:, theirs], 2, partner)
     load["w4"].wait()
     got4 = give(w4c.at[mine], w4c.at[theirs], 3, partner)
-
-    load["hcot"].wait()
-
-    def hot(src, dst, n, s):
-        return pltpu.make_async_remote_copy(
-            src_ref=src, dst_ref=dst, send_sem=hsend.at[n], recv_sem=hrecv.at[n],
-            device_id=(s, core), device_id_type=MESH,
-        )
-
-    @pl.loop(1, CHUNKS)
-    def _(j):
-        o = lax.rem(me + j, CHUNKS)
-        hot(rowmsg.at[o], rowbuf.at[me], 0, o).start()
-        hot(hc.at[o], carr.at[0, me], 1, o).start()
-
-    rowbuf[pl.ds(me, 1)] = rowmsg[pl.ds(me, 1)]
-    carr[0, pl.ds(me, 1)] = hc[pl.ds(me, 1)]
-
-    def hot_wait(ref, n, recv):
-        sem = (hrecv if recv else hsend).at[n]
-        part = ref.at[pl.ds(0, CHUNKS - 1)]
-        pltpu.make_async_copy(part, part, sem).wait()
-
-    def activate(pre, act, ds, columns):
-        sig = 0.5 * jnp.tanh(0.5 * pre) + 0.5
-        act[:, columns] = (pre * sig).astype(bf16)
-        ds[:, columns] = sig * (1.0 + pre * (1.0 - sig))
-
-    def layer(src, w, act, ds, lo, hi):
-        @pl.loop(lo, hi)
-        def _(n):
-            pre = jnp.dot(src[...], w[:, tile(n)], preferred_element_type=f32)
-            activate(pre, act, ds, tile(n))
-
-    layer(feats, w1c, a1, ds1, 0, 2)
-    got1.wait_recv()
-    layer(feats, w1c, a1, ds1, 2, 4)
+    got1[0].wait_recv()
+    layer(feats, w1c, a1, ds1, 2, 3)
+    got1[1].wait_recv()
+    layer(feats, w1c, a1, ds1, 3, 4)
     got2.wait_recv()
     layer(a1, w2c, a2, ds2, 0, 4)
     layer(a2, w3c, a3, ds3, 0, 2)
@@ -411,21 +415,22 @@
     got4.wait_recv()
     load["cot"].wait()
 
-    @pl.loop(0, 4)
-    def _(n):
-        b3[:, tile(n)] = (times_transposed(cot[...], w4c[tile(n), :]) * ds3[:, tile(n)]).astype(bf16)
+    def backward(src, w, ds, out):
+        for n in range(4):
+            columns = pl.ds(n * 256, 256)
+            out[:, columns] = (times_transposed(src[...], w[columns, :]) * ds[:, columns]).astype(bf16)
+
+    backward(cot, w4c, ds3, b3)
 
     def tall_grad(act, back, g, half, ref):
-        @pl.loop(0, 4)
-        def _(m):
-            t = rows_by_columns(act[:, tile(m)], back[:, pl.ds(half * MINE, MINE)])
+        for m in range(4):
+            t = rows_by_columns(act[:, pl.ds(m * 256, 256)], back[:, pl.ds(half * MINE, MINE)])
             ref[g][pl.ds(m * 16, 16)] = t.reshape(16, 16, 512).astype(ref[g].dtype)
 
     def wide_grad(half, ref):
-        @pl.loop(0, 2)
-        def _(m):
+        for m in range(2):
             for h in range(2):
-                t = rows_by_columns(a1[:, tile(m + 2 * half)], b2[:, pl.ds(h * 512, 512)])
+                t = rows_by_columns(a1[:, pl.ds((m + 2 * half) * 256, 256)], b2[:, pl.ds(h * 512, 512)])
                 ref[TWO][pl.ds(h * 32 + m * 16, 16)] = t.reshape(16, 16, 512).astype(ref[TWO].dtype)
 
     def grad_four(half, ref):
@@ -440,25 +445,19 @@
     grad_four(0, own)
     first.combine()
 
-    @pl.loop(0, 4)
-    def _(n):
-        b2[:, tile(n)] = (times_transposed(b3[...], w3c[tile(n), :]) * ds2[:, tile(n)]).astype(bf16)
+    backward(b3, w3c, ds2, b2)
 
     wide_grad(1, other)
     second.swap()
     first.relay()
     wide_grad(0, own)
+    backward(b2, w2c, ds1, b1)
     second.combine()
-
-    @pl.loop(0, 4)
-    def _(n):
-        b1[:, tile(n)] = (times_transposed(b2[...], w2c[tile(n), :]) * ds1[:, tile(n)]).astype(bf16)
-
     tall_grad(feats, b1, ONE, 1, other)
     third.swap()
     first.spread()
+    tall_grad(feats, b1, ONE, 0, own)
     second.relay()
-    tall_grad(feats, b1, ONE, 0, own)
     third.combine()
 
     emb[core] = jnp.dot(a3[...], w4c[...], preferred_element_type=f32).astype(bf16)
@@ -473,77 +472,83 @@
     got_rows = give(rowsum.at[0], rowsum.at[1], 5, partner)
     hot_wait(carr.at[0], 1, True)
     got_carr = give(carr.at[0], carr.at[1], 6, partner)
-    first.finish()
-    load["table"].wait()
-
-    @pl.loop(0, OWNED // WIDTH)
-    def _(n):
-        tabt[:, tile(n, WIDTH)] = jnp.transpose(tab[tile(n, WIDTH), :]).astype(bf16)
-
-    def select(which, block):
+
+    def select(which, block, into):
         row = lax.broadcasted_iota(i32, (ROWBLOCK, WIDTH), 0) + (block * ROWBLOCK + 1)
         for g in range(8):
             hit = row == jnp.broadcast_to(rowsum[which, g][0:1, :], (ROWBLOCK, WIDTH))
-            onehot[:, pl.ds(g * WIDTH, WIDTH)] = jnp.where(hit, 1.0, 0.0).astype(bf16)
-
+            into[:, pl.ds(g * WIDTH, WIDTH)] = jnp.where(hit, 1.0, 0.0).astype(bf16)
+
+    blocks = OWNED // ROWBLOCK
+    kept = core * (blocks // 2)
+
+    def fetch(lo, hi, update):
+        @pl.loop(lo, hi, step=2)
+        def _(n):
+            for k, hot_block in ((0, onehot), (1, twohot)):
+                block = lax.rem(kept + n + k, blocks)
+                where = tile(block, ROWBLOCK)
+                select(0, block, hot_block)
+                embt[...] += jnp.dot(tabt[:, where], hot_block[...], preferred_element_type=f32)
+                if update:
+                    delta = jnp.dot(
+                        hot_block[...], carr[0].reshape(ASKED, WIDTH), preferred_element_type=f32
+                    )
+                    newtab[where, :] = tab[where, :] - learn_rate * delta
+
+    def update(lo, hi):
+        @pl.loop(lo, hi, step=2)
+        def _(n):
+            for k, hot_block in ((0, onehot), (1, twohot)):
+                where = tile(kept + n + k, ROWBLOCK)
+                select(1, kept + n + k, hot_block)
+                delta = jnp.dot(
+                    hot_block[...], carr[1].reshape(ASKED, WIDTH), preferred_element_type=f32
+                )
+                newtab[where, :] = newtab[where, :] - learn_rate * delta
+
+    embt[...] = jnp.zeros_like(embt)
+    fetch(0, 2, True)
     second.spread()
     third.relay()
-    embt[...] = jnp.zeros_like(embt)
-
-    @pl.loop(0, OWNED // ROWBLOCK)
-    def _(n):
-        select(0, n)
-        embt[...] += jnp.dot(tabt[:, tile(n, ROWBLOCK)], onehot[...], preferred_element_type=f32)
+    fetch(2, 4, True)
+    first.finish()
+    third.spread()
+    fetch(4, 6, False)
+    fetch(6, 8, False)
 
     for g in range(8):
         found = jnp.transpose(embt[:, pl.ds(g * WIDTH, WIDTH)]).astype(bf16)
         ebuf[pl.ds(g * 8, 8)] = found.reshape(8, SPAN, WIDTH)
 
-    @pl.loop(1, CHUNKS)
+    @pl.loop(1, CHUNKS, unroll=7)
     def _(j):
         s = lax.rem(me + j, CHUNKS)
         hot(ebuf.at[s], hout.at[me, core], 2, s).start()
 
     hout[pl.ds(me, 1), pl.ds(core, 1)] = ebuf[pl.ds(me, 1)][:, None]
 
-    first.share()
     second.finish()
-    third.spread()
     got_rows.wait_recv()
     got_carr.wait_recv()
-
-    def update(lo, hi):
-        @pl.loop(lo, hi)
-        def _(n):
-            rows = tile(n, ROWBLOCK)
-            select(0, n)
-            delta = jnp.dot(onehot[...], carr[0].reshape(ASKED, WIDTH), preferred_element_type=f32)
-            select(1, n)
-            delta += jnp.dot(onehot[...], carr[1].reshape(ASKED, WIDTH), preferred_element_type=f32)
-            newtab[rows, :] = tab[rows, :] - learn_rate * delta
-
     update(0, 2)
+    first.share()
+    third.finish()
+    update(2, 4)
+    half = tile(core, OWNED // 2)
+    got_table = give(newtab.at[half], newtab.at[half], 8, partner)
     first.forward()
     second.share()
-    third.finish()
-    update(2, 4)
+    second.forward()
     first.close()
-    second.forward()
     third.share()
-    update(4, 6)
-    third.forward()
     hot_wait(hout.at[:, 0], 2, True)
     got_hot = give(hout.at[:, core], hout.at[:, core], 7, partner)
-    update(6, 8)
-    put_table = pltpu.make_async_copy(newtab, table_out, stores.at[0])
-    put_table.start()
+    third.forward()
     second.close()
     got_emb.wait_recv()
-    put_emb = pltpu.make_async_copy(emb, emb_out, stores.at[1])
-    put_emb.start()
+    got_table.wait_recv()
     got_hot.wait_recv()
-    put_hot = pltpu.make_async_copy(hout, hot_out, stores.at[2])
-    put_hot.start()
     third.close()
 
     for group in (first, second, third):
@@ -553,8 +558,6 @@
     hot_wait(rowbuf, 0, False)
     hot_wait(carr.at[0], 1, False)
     hot_wait(ebuf, 2, False)
-    for c in (put_table, put_emb, put_hot):
-        c.wait()
 
 
 def shapes(count, types=TYPES):
@@ -580,11 +583,10 @@
             jax.ShapeDtypeStruct((OWNED, WIDTH), f32),
             jax.ShapeDtypeStruct((2, TOKENS, WIDTH), bf16),
         ],
-        in_specs=[vmem] * 4 + [anywhere] * 7,
-        out_specs=[anywhere] * 7,
+        in_specs=[anywhere] * 12,
+        out_specs=[vmem] * 7,
         scratch_shapes=(
-            shapes(CHUNKS, (f32,) * 4)
-            + shapes(CHUNKS)
+            shapes(CHUNKS)
             + shapes(CHUNKS)
             + shapes(CHUNKS)
             + shapes(PLANE)
@@ -592,58 +594,99 @@
             + shapes(PLANE)
             + shapes(PLANE - 1)
             + shapes(1)
-            + outs(pltpu.VMEM)
-            + [dma((len(STREAMS), SLOTS)), dma((len(STREAMS), SLOTS)), dma((len(STREAMS), 2))]
+            + [dma((len(STREAMS), SLOTS)), dma((len(STREAMS), SLOTS))]
+            + [pltpu.VMEM((CHUNKS, 16, 512), f32), pltpu.VMEM((CHUNKS, 8, WIDTH), f32)]
             + [pltpu.VMEM(square, bf16)] * 3
             + [pltpu.VMEM((HIDDEN, WIDTH), bf16)]
             + [pltpu.VMEM(tokens, bf16)] * 4
             + [pltpu.VMEM(tokens, f32)] * 3
-            + [pltpu.VMEM(tokens, bf16)] * 3
+            + [pltpu.VMEM(tokens, bf16)] * 2
             + [
                 pltpu.VMEM((TOKENS, WIDTH), bf16),
-                pltpu.VMEM((2, TOKENS, WIDTH), bf16),
                 pltpu.VMEM((OWNED, WIDTH), f32),
                 pltpu.VMEM((WIDTH, OWNED), bf16),
-                pltpu.VMEM((OWNED, WIDTH), f32),
+                pltpu.VMEM((WIDTH, WIDTH), i32),
                 pltpu.VMEM((CHUNKS, 8, WIDTH), i32),
                 pltpu.VMEM((CHUNKS, 8, WIDTH), i32),
                 pltpu.VMEM((2, 8, 8, WIDTH), i32),
                 pltpu.VMEM((CHUNKS, SPAN, WIDTH), bf16),
                 pltpu.VMEM((2, CHUNKS, SPAN, WIDTH), bf16),
                 pltpu.VMEM((ROWBLOCK, ASKED), bf16),
+                pltpu.VMEM((ROWBLOCK, ASKED), bf16),
                 pltpu.VMEM((WIDTH, ASKED), f32),
                 pltpu.VMEM((CHUNKS, SPAN, WIDTH), bf16),
-                pltpu.VMEM((CHUNKS, 2, SPAN, WIDTH), bf16),
-                dma((7,)), dma((8,)), dma((8,)), dma((3,)), dma((3,)), dma((3,)),
+                dma((12,)), dma((10,)), dma((10,)), dma((3,)), dma((3,)),
+                pltpu.VMEM((1, 2 * SPAN, CHUNKS), i32),
+                pltpu.VMEM((1, CHUNKS), i32),
+                pltpu.VMEM((8, WIDTH), i32),
+                pltpu.VMEM((8, WIDTH), i32),
+                pltpu.VMEM((8, WIDTH), i32),
             ]
         ),
         compiler_params=pltpu.CompilerParams(
-            collective_id=0, has_side_effects=True, vmem_limit_bytes=67043328
+            collective_id=0, has_side_effects=True, vmem_limit_bytes=43 * 1024 * 1024
         ),
         name="step",
-    )(*args)
+    )(*(pltpu.with_memory_space_constraint(a, pltpu.HBM) for a in args))
+
+
+def deliver(results, factor):
+    vmem = pl.BlockSpec(memory_space=pltpu.VMEM)
+    pieces = 4
+
+    def kernel(*refs):
+        sources, targets, stages, sem = refs[:7], refs[7:14], refs[14:18], refs[18]
+        copies = []
+
+        def put(src, dst):
+            c = pltpu.make_async_copy(src, dst, sem.at[len(copies)])
+            c.start()
+            copies.append(c)
+
+        for src, dst in zip(sources[4:], targets[4:]):
+            put(src, dst)
+        for src, dst, stage in zip(sources, targets, stages):
+            n = src.shape[0] // pieces
+            for i in range(pieces):
+                part = pl.ds(i * n, n)
+                stage[part] = src[part].astype(f32) * factor
+                put(stage.at[part], dst.at[part])
+        for c in copies:
+            c.wait()
+
+    return pl.pallas_call(
+        kernel,
+        out_shape=[
+            jax.ShapeDtypeStruct(r.shape, f32 if i < 4 else r.dtype) for i, r in enumerate(results)
+        ],
+        in_specs=[vmem] * 7,
+        out_specs=[pl.BlockSpec(memory_space=pl.ANY)] * 7,
+        scratch_shapes=[pltpu.VMEM(r.shape, f32) for r in results[:4]]
+        + [pltpu.SemaphoreType.DMA((3 + 4 * pieces,))],
+        compiler_params=pltpu.CompilerParams(vmem_limit_bytes=16 * 1024 * 1024),
+        name="deliver",
+    )(*results)
 
 
 def local(
     hot_rows, hot_count, hot_cot, table, cold_ids, hash_mult, hash_add,
     layer_one, layer_two, layer_three, layer_four, cold_cot,
 ):
-    slots = jnp.arange(hot_rows.shape[2], dtype=i32)
-    asked = jnp.where(slots[None, :] < hot_count[0][:, None], hot_rows[0] + 1, 0)
-    asked = jnp.pad(asked, ((0, 0), (0, WIDTH - asked.shape[1])))
-    r3, r4, r2, r1, hot_emb, new_table, cold_emb = step(
-        asked, cold_ids.reshape(8, WIDTH), hash_mult.reshape(8, WIDTH), hash_add.reshape(8, WIDTH),
+    results = step(
+        hot_rows.transpose(0, 2, 1), hot_count, cold_ids.reshape(8, WIDTH),
+        hash_mult.reshape(8, WIDTH), hash_add.reshape(8, WIDTH),
         layer_one, layer_two, layer_three, layer_four, cold_cot, hot_cot, table,
     )
     factor = float(cold_ids.shape[0] * lax.axis_size("dp")) ** (-0.5)
+    g3, g4, g2, g1, hot_emb, new_table, cold_emb = deliver(results, factor)
     return (
         hot_emb.reshape(hot_cot.shape),
         new_table,
         cold_emb.reshape(cold_cot.shape),
-        r1.reshape(layer_one.shape).astype(f32) * factor,
-        r2.reshape(layer_two.shape).astype(f32) * factor,
-        r3.reshape(layer_three.shape).astype(f32) * factor,
-        r4.reshape(layer_four.shape) * factor,
+        g1.reshape(layer_one.shape),
+        g2.reshape(layer_two.shape),
+        g3.reshape(layer_three.shape),
+        g4.reshape(layer_four.shape),
     )
 
 

time: 91.6 us -> 75.7 us (0.83)
  other arithmetic: 7.33 us -> 0 us
  Pallas kernels: 79.1 us -> 74.7 us
  local copies, waits for them, and re-layouts: 4.26 us -> 0 us
    pallas_call x1, Pallas kernels: 79.1 us -> 71 us  [step(): pl.pallas_call(step_kernel, out_shape=outs(jax.ShapeDtypeStruct) + [jax.S...]
    mul x3 -> x0, other arithmetic: 6.6 us -> none  [the longest x1 4.28 us: local(): r3.reshape(layer_three.shape).astype(f32) * factor]
    pallas_call x0 -> x1, Pallas kernels: none -> 3.77 us  [deliver(): pl.pallas_call(kernel, out_shape=[jax.ShapeDtypeStruct(r.shape, f32 if i...]
    unnamed x14 -> x0, local copies, waits for them, and re-layouts: 3.63 us -> none
where the time goes in v3:
time: 75.7 us; the launch traced here: 75.5 us
  Pallas kernels  74.7 us (99%)
  between operations  0.81 us (1%)
    pallas_call x1, Pallas kernels, step(): pl.pallas_call(step_kernel, out_shape=outs(jax.ShapeDtypeStruct) + [jax.S...  71 us
    pallas_call x1, Pallas kernels, deliver(): pl.pallas_call(kernel, out_shape=[jax.ShapeDtypeStruct(r.shape, f32 if i...  3.77 us

profile of v3, /device:TPU:0, one launch (start us, length us, event | category | flops | bytes accessed | tf_op | source)
XLA Modules:
  0.0 75.5 jit_solution(14224676697058765170)
XLA Ops:
  0.6 71.0 %step.1 = (bf16[64,16,512]{2,1,0:T(8,128)(2,1)S(1)}, f32[64,8,128]{2,1,0:T(8,128)S(1)}, bf16[32,16,1024]{2,1,0:T(8,128)(2,1)S(1)}, bf16[64,16,512]{2,1,0:T(8,128...) custom-call(s32[1,32,64]{2,1,0:T(8,128)} %bitcast.10, ...), custom_call_target="tpu_custom_call" | custom-call | tf_op jit(solution)/shard_map/step/pallas_call | solution.py:579
  71.6 3.8 %deliver.1 = (f32[64,16,512]{2,1,0:T(8,128)}, f32[64,8,128]{2,1,0:T(8,128)}, f32[32,16,1024]{2,1,0:T(8,128)}, f32[64,16,512]{2,1,0:T(8,128)}, bf16[64,2,16,128]{...) custom-call(bf16[64,16,512]{2,1,0:T(8,128)(2,1)S(1)} %get-tuple-element.21.refs_0_, ...), custom_call_target="tpu_custom_call" | custom-call | tf_op jit(solution)/shard_map/deliver/pallas_call | solution.py:657

commit v4 on v3

--- a/solution.py
+++ b/solution.py
@@ -25,7 +25,8 @@
 THREE, FOUR, TWO, ONE = range(4)
 LANES = (512, 128, 512, 512)
 ROWS = (16, 8, 16, 16)
-TYPES = (bf16, f32, bf16, bf16)
+TYPES = (bf16,) * 4
+DIRECT = (ONE,)
 STREAMS = (
     (THREE, 0, 2, 0),
     (THREE, 2, 1, 1),
@@ -38,7 +39,7 @@
     (ONE, 2, 1, 0),
     (ONE, 3, 1, 1),
 )
-SLOTS = 15
+SLOTS = 17
 
 
 class Place:
@@ -58,6 +59,11 @@
         self.right = me + (self.after - self.k) * self.stride
         self.left = me + (self.before - self.k) * self.stride
 
+    def along(self, axis, j):
+        at = self.second if axis else self.first
+        to = lax.rem(at + j, RING)
+        return lax.axis_index("dp") + (to - at) * self.others[axis], to
+
     def peer(self, p):
         return (
             self.k * self.stride
@@ -74,7 +80,7 @@
         self.lanes = pl.ds(b0 * WIDTH, nb * WIDTH)
         self.lane0, self.nlanes = b0 * WIDTH, nb * WIDTH
         g = self.grad
-        for name in ("own", "other", "arrive", "total", "out", "near", "side", "part", "fan", "final"):
+        for name in ("own", "other", "arrive", "total", "out", "near", "side", "part", "fan"):
             setattr(self, name, refs[name][g])
         self.send, self.recv = refs["send"], refs["recv"]
         self.dtype = TYPES[g]
@@ -179,38 +185,79 @@
                 + self.load(self.side, PLANE + i * 4, 4),
             )
 
-        @pl.loop(1, PLANE, unroll=5)
-        def _(j):
-            p = lax.rem(q.p + j, PLANE)
+        if self.grad in DIRECT:
+            @pl.loop(1, PLANE, unroll=5)
+            def _(j):
+                p = lax.rem(q.p + j, PLANE)
+                self.copy(
+                    self.view(self.part, p, 1), self.view(self.fan, j - 1, 1), 7, (q.peer(p), q.core)
+                ).start()
+        else:
+            for j in range(1, RING):
+                dp, to = q.along(0, j)
+                self.copy(
+                    self.view(self.part, to * RING, RING), self.view(self.fan, (j - 1) * RING, RING),
+                    7, (dp, q.core),
+                ).start()
+
+    def middle(self):
+        if self.grad in DIRECT:
+            return
+        q = self.place
+        self.wait_chunks(7, 12, True)
+        mine = q.first * RING
+        acc = self.load(self.part, mine, RING)
+        for j in range(3):
+            acc = acc + self.load(self.fan, j * RING, RING)
+        self.store(self.part, mine, RING, acc)
+        for j in range(1, RING):
+            dp, to = q.along(1, j)
             self.copy(
-                self.view(self.part, p, 1), self.view(self.fan, j - 1, 1), 7, (q.peer(p), q.core)
+                self.view(self.part, mine + to, 1), self.view(self.fan, 11 + j, 1), 15, (dp, q.core)
             ).start()
 
-    def wait_fan(self, slot, recv):
-        fifteen = self.view(self.fan, 0, PLANE - 1)
+    def wait_chunks(self, slot, count, recv):
+        some = self.view(self.fan, 0, count)
         sem = (self.recv if recv else self.send).at[self.index, slot]
-        pltpu.make_async_copy(fifteen, fifteen, sem).wait()
+        pltpu.make_async_copy(some, some, sem).wait()
 
     def finish(self):
         q = self.place
-        self.wait_fan(7, True)
+        direct = self.grad in DIRECT
+        if direct:
+            self.wait_chunks(7, 15, True)
+        else:
+            self.wait_chunks(15, 3, True)
         acc = self.load(self.part, q.p, 1)
-        for i in range(PLANE - 1):
+        for i in range(0 if direct else 12, PLANE - 1):
             acc = acc + self.load(self.fan, i, 1)
-        self.store(self.final, 0, 1, acc)
         here = q.k * PLANE + q.p
-        self.outview(self.out, here, 1)[...] = acc.astype(self.dtype)
-
-        @pl.loop(1, PLANE, unroll=5)
-        def _(j):
-            p = lax.rem(q.p + j, PLANE)
-            self.copy(
-                self.view(self.final, 0, 1), self.outview(self.out, here, 1), 8, (q.peer(p), q.core)
-            ).start()
+        result = self.outview(self.out, here, 1)
+        result[...] = acc.astype(self.dtype)
+        if direct:
+            @pl.loop(1, PLANE, unroll=5)
+            def _(j):
+                p = lax.rem(q.p + j, PLANE)
+                self.copy(result, result, 8, (q.peer(p), q.core)).start()
+        else:
+            for j in range(1, RING):
+                self.copy(result, result, 8, (q.along(1, j)[0], q.core)).start()
+
+    def collect(self):
+        if self.grad in DIRECT:
+            return
+        q = self.place
+        self.wait_chunks(8, 3, True)
+        four = self.outview(self.out, q.k * PLANE + q.first * RING, RING)
+        for j in range(1, RING):
+            self.copy(four, four, 16, (q.along(0, j)[0], q.core)).start()
 
     def share(self):
         q = self.place
-        self.wait_fan(8, True)
+        if self.grad in DIRECT:
+            self.wait_chunks(8, 15, True)
+        else:
+            self.wait_chunks(16, 12, True)
         low = self.outview(self.out, q.k * PLANE, HALF)
         high = self.outview(self.out, q.k * PLANE + HALF, HALF)
         self.c_gl = self.start(low, low, 9, dp=q.right)
@@ -234,8 +281,12 @@
     def drain(self):
         for c in self.pending:
             c.wait_send()
-        self.wait_fan(7, False)
-        self.wait_fan(8, False)
+        if self.grad in DIRECT:
+            counts = ((7, 15), (8, 15))
+        else:
+            counts = ((7, 12), (15, 3), (8, 3), (16, 12))
+        for slot, count in counts:
+            self.wait_chunks(slot, count, False)
 
 
 class Group:
@@ -266,7 +317,7 @@
     r3, r4, r2, r1, hout, newtab, emb,
     *rest,
 ):
-    names = ("other", "arrive", "total", "near", "side", "part", "fan", "final")
+    names = ("other", "arrive", "total", "near", "side", "part", "fan")
     refs = {name: rest[4 * i : 4 * i + 4] for i, name in enumerate(names)}
     rest = rest[4 * len(names) :]
     (
@@ -365,23 +416,6 @@
     def _(n):
         tabt[:, tile(n, WIDTH)] = jnp.transpose(tab[tile(n, WIDTH), :]).astype(bf16)
 
-    load["hcot"].wait()
-
-    def hot(src, dst, n, s):
-        return pltpu.make_async_remote_copy(
-            src_ref=src, dst_ref=dst, send_sem=hsend.at[n], recv_sem=hrecv.at[n],
-            device_id=(s, core), device_id_type=MESH,
-        )
-
-    @pl.loop(1, CHUNKS, unroll=7)
-    def _(j):
-        o = lax.rem(me + j, CHUNKS)
-        hot(rowmsg.at[o], rowbuf.at[me], 0, o).start()
-        hot(hc.at[o], carr.at[0, me], 1, o).start()
-
-    rowbuf[pl.ds(me, 1)] = rowmsg[pl.ds(me, 1)]
-    carr[0, pl.ds(me, 1)] = hc[pl.ds(me, 1)]
-
     def hot_wait(ref, n, recv):
         sem = (hrecv if recv else hsend).at[n]
         part = ref.at[pl.ds(0, CHUNKS - 1)]
@@ -390,7 +424,7 @@
     def activate(pre, act, ds, columns):
         sig = 0.5 * jnp.tanh(0.5 * pre) + 0.5
         act[:, columns] = (pre * sig).astype(bf16)
-        ds[:, columns] = sig * (1.0 + pre * (1.0 - sig))
+        ds[:, columns] = sig + (pre * sig) * (1.0 - sig)
 
     def layer(src, w, act, ds, lo, hi):
         for n in range(lo, hi):
@@ -407,6 +441,24 @@
     layer(feats, w1c, a1, ds1, 2, 3)
     got1[1].wait_recv()
     layer(feats, w1c, a1, ds1, 3, 4)
+
+    load["hcot"].wait()
+
+    def hot(src, dst, n, s):
+        return pltpu.make_async_remote_copy(
+            src_ref=src, dst_ref=dst, send_sem=hsend.at[n], recv_sem=hrecv.at[n],
+            device_id=(s, core), device_id_type=MESH,
+        )
+
+    @pl.loop(1, CHUNKS, unroll=7)
+    def _(j):
+        o = lax.rem(me + j, CHUNKS)
+        hot(rowmsg.at[o], rowbuf.at[me], 0, o).start()
+        hot(hc.at[o], carr.at[0, me], 1, o).start()
+
+    rowbuf[pl.ds(me, 1)] = rowmsg[pl.ds(me, 1)]
+    carr[0, pl.ds(me, 1)] = hc[pl.ds(me, 1)]
+
     got2.wait_recv()
     layer(a1, w2c, a2, ds2, 0, 4)
     layer(a2, w3c, a3, ds3, 0, 2)
@@ -435,7 +487,7 @@
 
     def grad_four(half, ref):
         t = rows_by_columns(a3[:, pl.ds(half * MINE, MINE)], cot[...])
-        ref[FOUR][...] = t.reshape(CHUNKS, 8, WIDTH)
+        ref[FOUR][...] = t.reshape(CHUNKS, 8, WIDTH).astype(ref[FOUR].dtype)
 
     own, other = refs["own"], refs["other"]
     tall_grad(a2, b3, THREE, 1, other)
@@ -443,25 +495,23 @@
     first.swap()
     tall_grad(a2, b3, THREE, 0, own)
     grad_four(0, own)
+    backward(b3, w3c, ds2, b2)
     first.combine()
-
-    backward(b3, w3c, ds2, b2)
-
     wide_grad(1, other)
     second.swap()
-    first.relay()
     wide_grad(0, own)
     backward(b2, w2c, ds1, b1)
+    first.relay()
     second.combine()
     tall_grad(feats, b1, ONE, 1, other)
     third.swap()
+    tall_grad(feats, b1, ONE, 0, own)
+
+    emb[core] = jnp.dot(a3[...], w4c[...], preferred_element_type=f32).astype(bf16)
+    got_emb = give(emb.at[core], emb.at[core], 4, partner)
     first.spread()
-    tall_grad(feats, b1, ONE, 0, own)
     second.relay()
     third.combine()
-
-    emb[core] = jnp.dot(a3[...], w4c[...], preferred_element_type=f32).astype(bf16)
-    got_emb = give(emb.at[core], emb.at[core], 4, partner)
 
     hot_wait(rowbuf, 0, True)
     for g in range(8):
@@ -509,12 +559,14 @@
 
     embt[...] = jnp.zeros_like(embt)
     fetch(0, 2, True)
+    first.middle()
     second.spread()
     third.relay()
     fetch(2, 4, True)
+    fetch(4, 6, False)
     first.finish()
+    second.middle()
     third.spread()
-    fetch(4, 6, False)
     fetch(6, 8, False)
 
     for g in range(8):
@@ -529,22 +581,24 @@
     hout[pl.ds(me, 1), pl.ds(core, 1)] = ebuf[pl.ds(me, 1)][:, None]
 
     second.finish()
+    first.collect()
     got_rows.wait_recv()
     got_carr.wait_recv()
     update(0, 2)
+    third.finish()
+    second.collect()
     first.share()
-    third.finish()
     update(2, 4)
     half = tile(core, OWNED // 2)
     got_table = give(newtab.at[half], newtab.at[half], 8, partner)
+    second.share()
     first.forward()
-    second.share()
-    second.forward()
-    first.close()
     third.share()
     hot_wait(hout.at[:, 0], 2, True)
     got_hot = give(hout.at[:, core], hout.at[:, core], 7, partner)
+    second.forward()
     third.forward()
+    first.close()
     second.close()
     got_emb.wait_recv()
     got_table.wait_recv()
@@ -593,7 +647,6 @@
             + shapes(2 * PLANE)
             + shapes(PLANE)
             + shapes(PLANE - 1)
-            + shapes(1)
             + [dma((len(STREAMS), SLOTS)), dma((len(STREAMS), SLOTS))]
             + [pltpu.VMEM((CHUNKS, 16, 512), f32), pltpu.VMEM((CHUNKS, 8, WIDTH), f32)]
             + [pltpu.VMEM(square, bf16)] * 3

time: 75.7 us -> 68.7 us (0.908)
  Pallas kernels: 74.7 us -> 67.8 us
    pallas_call x1, Pallas kernels: 71 us -> 64 us  [step(): pl.pallas_call(step_kernel, out_shape=outs(jax.ShapeDtypeStruct) + [jax.S...]
where the time goes in v4:
time: 68.7 us; the launch traced here: 68.6 us
  Pallas kernels  67.8 us (99%)
  between operations  0.81 us (1%)
    pallas_call x1, Pallas kernels, step(): pl.pallas_call(step_kernel, out_shape=outs(jax.ShapeDtypeStruct) + [jax.S...  64 us
    pallas_call x1, Pallas kernels, deliver(): pl.pallas_call(kernel, out_shape=[jax.ShapeDtypeStruct(r.shape, f32 if i...  3.77 us

profile of v4, /device:TPU:0, one launch (start us, length us, event | category | flops | bytes accessed | tf_op | source)
XLA Modules:
  0.0 68.6 jit_solution(16220421402925711844)
XLA Ops:
  0.6 64.0 %step.1 = (bf16[64,16,512]{2,1,0:T(8,128)(2,1)S(1)}, bf16[64,8,128]{2,1,0:T(8,128)(2,1)S(1)}, bf16[32,16,1024]{2,1,0:T(8,128)(2,1)S(1)}, bf16[64,16,512]{2,1,0:T...) custom-call(s32[1,32,64]{2,1,0:T(8,128)} %bitcast.10, ...), custom_call_target="tpu_custom_call" | custom-call | tf_op jit(solution)/shard_map/step/pallas_call | solution.py:633
  64.7 3.8 %deliver.1 = (f32[64,16,512]{2,1,0:T(8,128)}, f32[64,8,128]{2,1,0:T(8,128)}, f32[32,16,1024]{2,1,0:T(8,128)}, f32[64,16,512]{2,1,0:T(8,128)}, bf16[64,2,16,128]{...) custom-call(bf16[64,16,512]{2,1,0:T(8,128)(2,1)S(1)} %get-tuple-element.21.refs_0_, ...), custom_call_target="tpu_custom_call" | custom-call | tf_op jit(solution)/shard_map/deliver/pallas_call | solution.py:710

commit v5 on v4

--- a/solution.py
+++ b/solution.py
@@ -374,12 +374,12 @@
     want = jnp.transpose(spare[...])[:CHUNKS]
     rowmsg[...] = jnp.broadcast_to(want[:, None, :], (CHUNKS, 8, WIDTH))
 
-    for b in range(TOKENS // WIDTH):
+    def hash_block(b):
         line = ids[pl.ds(core * (TOKENS // WIDTH) + b, 1), :]
         column = jnp.transpose(jnp.broadcast_to(line, (WIDTH, WIDTH)))
 
         @pl.loop(0, HIDDEN // WIDTH, unroll=2)
-        def _(j, b=b, column=column):
+        def _(j):
             h = column * mult[pl.ds(j, 1), :] + add[pl.ds(j, 1), :]
             q = (h.astype(f32) * ((1.0 - 4e-7) / modulus)).astype(i32)
             r = h - q * modulus
@@ -388,6 +388,8 @@
                 r.astype(f32) * (2.0 / 1000002.0) - 1.0
             ).astype(bf16)
 
+    hash_block(0)
+    hash_block(1)
     pl.semaphore_wait(barrier, CHUNKS)
 
     sent = []
@@ -409,34 +411,41 @@
     ]
     load["w2"].wait()
     got2 = give(w2c.at[mine], w2c.at[theirs], 9, partner)
-
-    load["table"].wait()
-
-    @pl.loop(0, OWNED // WIDTH, unroll=8)
-    def _(n):
-        tabt[:, tile(n, WIDTH)] = jnp.transpose(tab[tile(n, WIDTH), :]).astype(bf16)
+    hash_block(2)
+    hash_block(3)
 
     def hot_wait(ref, n, recv):
         sem = (hrecv if recv else hsend).at[n]
         part = ref.at[pl.ds(0, CHUNKS - 1)]
         pltpu.make_async_copy(part, part, sem).wait()
 
-    def activate(pre, act, ds, columns):
+    def activate(pre, act, ds, rows, columns):
         sig = 0.5 * jnp.tanh(0.5 * pre) + 0.5
-        act[:, columns] = (pre * sig).astype(bf16)
-        ds[:, columns] = sig + (pre * sig) * (1.0 - sig)
+        act[rows, columns] = (pre * sig).astype(bf16)
+        ds[rows, columns] = sig + (pre * sig) * (1.0 - sig)
 
     def layer(src, w, act, ds, lo, hi):
+        last = None
         for n in range(lo, hi):
-            columns = pl.ds(n * 256, 256)
-            pre = jnp.dot(src[...], w[:, columns], preferred_element_type=f32)
-            activate(pre, act, ds, columns)
+            for h in range(2):
+                at = (pl.ds(h * 256, 256), pl.ds(n * 256, 256))
+                pre = jnp.dot(src[at[0], :], w[:, at[1]], preferred_element_type=f32)
+                if last is not None:
+                    activate(last[0], act, ds, *last[1])
+                last = (pre, at)
+        activate(last[0], act, ds, *last[1])
 
     layer(feats, w1c, a1, ds1, 0, 2)
     load["w3"].wait()
     got3 = give(w3c.at[:, mine], w3c.at[:, theirs], 2, partner)
     load["w4"].wait()
     got4 = give(w4c.at[mine], w4c.at[theirs], 3, partner)
+    load["table"].wait()
+
+    @pl.loop(0, OWNED // WIDTH, unroll=8)
+    def _(n):
+        tabt[:, tile(n, WIDTH)] = jnp.transpose(tab[tile(n, WIDTH), :]).astype(bf16)
+
     got1[0].wait_recv()
     layer(feats, w1c, a1, ds1, 2, 3)
     got1[1].wait_recv()
@@ -485,16 +494,18 @@
                 t = rows_by_columns(a1[:, pl.ds((m + 2 * half) * 256, 256)], b2[:, pl.ds(h * 512, 512)])
                 ref[TWO][pl.ds(h * 32 + m * 16, 16)] = t.reshape(16, 16, 512).astype(ref[TWO].dtype)
 
-    def grad_four(half, ref):
-        t = rows_by_columns(a3[:, pl.ds(half * MINE, MINE)], cot[...])
-        ref[FOUR][...] = t.reshape(CHUNKS, 8, WIDTH).astype(ref[FOUR].dtype)
+    def grad_four():
+        t = rows_by_columns(cot[...], a3[...])
+        for half, ref in ((1, other), (0, own)):
+            part = jnp.transpose(t[:, half * MINE : (half + 1) * MINE])
+            ref[FOUR][...] = part.reshape(CHUNKS, 8, WIDTH).astype(ref[FOUR].dtype)
 
     own, other = refs["own"], refs["other"]
     tall_grad(a2, b3, THREE, 1, other)
-    grad_four(1, other)
-    first.swap()
+    Group(streams[:3]).swap()
+    grad_four()
+    streams[3].swap()
     tall_grad(a2, b3, THREE, 0, own)
-    grad_four(0, own)
     backward(b3, w3c, ds2, b2)
     first.combine()
     wide_grad(1, other)

time: 68.7 us -> 68.8 us (level)
  no operation moved by 1% of the time
where the time goes in v5:
time: 68.8 us; the launch traced here: 68.7 us
  Pallas kernels  67.9 us (99%)
  between operations  0.81 us (1%)
    pallas_call x1, Pallas kernels, step(): pl.pallas_call(step_kernel, out_shape=outs(jax.ShapeDtypeStruct) + [jax.S...  64.1 us
    pallas_call x1, Pallas kernels, deliver(): pl.pallas_call(kernel, out_shape=[jax.ShapeDtypeStruct(r.shape, f32 if i...  3.77 us

profile of v5, /device:TPU:0, one launch (start us, length us, event | category | flops | bytes accessed | tf_op | source)
XLA Modules:
  0.0 68.7 jit_solution(5205831853923948057)
XLA Ops:
  0.6 64.1 %step.1 = (bf16[64,16,512]{2,1,0:T(8,128)(2,1)S(1)}, bf16[64,8,128]{2,1,0:T(8,128)(2,1)S(1)}, bf16[32,16,1024]{2,1,0:T(8,128)(2,1)S(1)}, bf16[64,16,512]{2,1,0:T...) custom-call(s32[1,32,64]{2,1,0:T(8,128)} %bitcast.10, ...), custom_call_target="tpu_custom_call" | custom-call | tf_op jit(solution)/shard_map/step/pallas_call | solution.py:644
  64.7 3.8 %deliver.1 = (f32[64,16,512]{2,1,0:T(8,128)}, f32[64,8,128]{2,1,0:T(8,128)}, f32[32,16,1024]{2,1,0:T(8,128)}, f32[64,16,512]{2,1,0:T(8,128)}, bf16[64,2,16,128]{...) custom-call(bf16[64,16,512]{2,1,0:T(8,128)(2,1)S(1)} %get-tuple-element.21.refs_0_, ...), custom_call_target="tpu_custom_call" | custom-call | tf_op jit(solution)/shard_map/deliver/pallas_call | solution.py:721

commit v6 on v5

--- a/solution.py
+++ b/solution.py
@@ -39,7 +39,7 @@
     (ONE, 2, 1, 0),
     (ONE, 3, 1, 1),
 )
-SLOTS = 17
+SLOTS = 18
 
 
 class Place:
@@ -85,6 +85,7 @@
         self.send, self.recv = refs["send"], refs["recv"]
         self.dtype = TYPES[g]
         self.pending = []
+        self.swaps = []
 
     def view(self, ref, first, count):
         return ref.at[pl.ds(first, count), :, self.lanes]
@@ -120,13 +121,23 @@
         return c
 
     def swap(self):
-        self.c_swap = self.start(
-            self.view(self.other, 0, CHUNKS), self.view(self.arrive, 0, CHUNKS), 0,
+        self.swap_rows(0, CHUNKS, 0)
+
+    def swap_low(self):
+        self.swap_rows(0, CHUNKS // 2, 0)
+
+    def swap_high(self):
+        self.swap_rows(CHUNKS // 2, CHUNKS // 2, 17)
+
+    def swap_rows(self, first, count, slot):
+        self.swaps.append(self.start(
+            self.view(self.other, first, count), self.view(self.arrive, first, count), slot,
             mp=1 - self.place.core,
-        )
+        ))
 
     def combine(self):
-        self.c_swap.wait_recv()
+        for c in self.swaps:
+            c.wait_recv()
 
         @pl.loop(0, CHUNKS // 8, unroll=2)
         def _(i):
@@ -483,8 +494,8 @@
 
     backward(cot, w4c, ds3, b3)
 
-    def tall_grad(act, back, g, half, ref):
-        for m in range(4):
+    def tall_grad(act, back, g, half, ref, lo=0, hi=4):
+        for m in range(lo, hi):
             t = rows_by_columns(act[:, pl.ds(m * 256, 256)], back[:, pl.ds(half * MINE, MINE)])
             ref[g][pl.ds(m * 16, 16)] = t.reshape(16, 16, 512).astype(ref[g].dtype)
 
@@ -514,8 +525,10 @@
     backward(b2, w2c, ds1, b1)
     first.relay()
     second.combine()
-    tall_grad(feats, b1, ONE, 1, other)
-    third.swap()
+    tall_grad(feats, b1, ONE, 1, other, 0, 2)
+    third.swap_low()
+    tall_grad(feats, b1, ONE, 1, other, 2, 4)
+    third.swap_high()
     tall_grad(feats, b1, ONE, 0, own)
 
     emb[core] = jnp.dot(a3[...], w4c[...], preferred_element_type=f32).astype(bf16)
@@ -584,6 +597,9 @@
         found = jnp.transpose(embt[:, pl.ds(g * WIDTH, WIDTH)]).astype(bf16)
         ebuf[pl.ds(g * 8, 8)] = found.reshape(8, SPAN, WIDTH)
 
+    second.finish()
+    first.collect()
+
     @pl.loop(1, CHUNKS, unroll=7)
     def _(j):
         s = lax.rem(me + j, CHUNKS)
@@ -591,8 +607,6 @@
 
     hout[pl.ds(me, 1), pl.ds(core, 1)] = ebuf[pl.ds(me, 1)][:, None]
 
-    second.finish()
-    first.collect()
     got_rows.wait_recv()
     got_carr.wait_recv()
     update(0, 2)

time: 68.8 us -> 68.8 us (level)
  no operation moved by 1% of the time
where the time goes in v6:
time: 68.8 us; the launch traced here: 68.6 us
  Pallas kernels  67.8 us (99%)
  between operations  0.81 us (1%)
    pallas_call x1, Pallas kernels, step(): pl.pallas_call(step_kernel, out_shape=outs(jax.ShapeDtypeStruct) + [jax.S...  64.1 us
    pallas_call x1, Pallas kernels, deliver(): pl.pallas_call(kernel, out_shape=[jax.ShapeDtypeStruct(r.shape, f32 if i...  3.77 us

profile of v6, /device:TPU:0, one launch (start us, length us, event | category | flops | bytes accessed | tf_op | source)
XLA Modules:
  0.0 68.6 jit_solution(6933330087623128975)
XLA Ops:
  0.6 64.1 %step.1 = (bf16[64,16,512]{2,1,0:T(8,128)(2,1)S(1)}, bf16[64,8,128]{2,1,0:T(8,128)(2,1)S(1)}, bf16[32,16,1024]{2,1,0:T(8,128)(2,1)S(1)}, bf16[64,16,512]{2,1,0:T...) custom-call(s32[1,32,64]{2,1,0:T(8,128)} %bitcast.10, ...), custom_call_target="tpu_custom_call" | custom-call | tf_op jit(solution)/shard_map/step/pallas_call | solution.py:658
  64.7 3.8 %deliver.1 = (f32[64,16,512]{2,1,0:T(8,128)}, f32[64,8,128]{2,1,0:T(8,128)}, f32[32,16,1024]{2,1,0:T(8,128)}, f32[64,16,512]{2,1,0:T(8,128)}, bf16[64,2,16,128]{...) custom-call(bf16[64,16,512]{2,1,0:T(8,128)(2,1)S(1)} %get-tuple-element.21.refs_0_, ...), custom_call_target="tpu_custom_call" | custom-call | tf_op jit(solution)/shard_map/deliver/pallas_call | solution.py:735
